TPU v7x, 32 devices: a whole 2x2x4 slice. The times are simulated.
32 devices in a mesh: grp: 1, tile: 16 (over z, x, core), mem: 2 (over y).
Axes of the slice: x: 2, y: 2, z: 4, core: 2. Of those that a mesh axis runs over, the one named last changes fastest.
Arguments:
- ens_coarse: bfloat16 [1, 80, 128, 64, 64], P('grp', 'mem', None, 'tile'), may hold values from -6 to 6
- col_interp: bfloat16 [128, 64], replicated, may hold values from -0.75 to 0.75
- row_weights: bfloat16 [3, 128], replicated, may hold values from 0.099609375 to 0.8984375
- ctrl_vec: float32 [1, 128, 128, 128], P('grp', None, 'tile'), may hold values from -24 to 24
- band_loc: bfloat16 [128, 24], P('tile'), may hold values from -1.25 to 1.25
- row_loc: bfloat16 [128, 128], replicated, may hold values from -0.5 to 0.5
- level_loc: bfloat16 [128, 128], replicated, may hold values from -0.5 to 0.5
- hx_pert: bfloat16 [1, 80, 65536], P('grp', None, ('tile', 'mem')), may hold values from -3 to 3
- innov: float32 [1, 65536], P('grp', ('tile', 'mem')), may hold values from -48 to 48
- obs_prec: float32 [1, 65536], P('grp', ('tile', 'mem')), may hold values from 0.3 to 3
- obs_region: int32 [1, 65536], P('grp', ('tile', 'mem')), may hold values from 0 to 7
Outputs:
- increment: float32 [1, 128, 128, 128], P('grp', 'mem', 'tile')
- letkf_weights: float32 [128, 80], P('tile')
Inputs may be any that keep to these rules, and one draw needn't show every extreme that they name: `obs_region`: the region of an observation among the 8 regions of its block of 4096 observations.
All inputs are finite; a program needn't handle non-finite values.
Results may differ from a plain program's by a relative error of at most 0.018.
Values may be sent and summed in bfloat16 or wider, within the bound.
A program may use at most 128 MiB of HBM per device.

v0:
```python
import jax
import jax.numpy as jnp
from jax import lax
from jax.experimental import pallas as pl
from jax.experimental.pallas import tpu as pltpu
from jax.sharding import PartitionSpec as P

NREG = 8
GROUP = 16
CHUNKS = 2


def extended(value, sides, width):
    for axis, dim in sides:
        peers, length = (lax.axis_size(axis), value.shape[dim])
        up = [(i, (i + 1) % peers) for i in range(peers - 1)]
        down = [(j, i) for i, j in up]
        last = lax.slice_in_dim(value, length - width, length, axis=dim)
        first = lax.slice_in_dim(value, 0, width, axis=dim)
        before = lax.ppermute(last, axis, up)
        after = lax.ppermute(first, axis, down)
        value = jnp.concatenate([before, value, after], axis=dim)
    return value


def swap_add(value):
    peers = lax.axis_size("mem")
    me = lax.axis_index("mem")
    length = value.shape[0] // peers
    total = lax.dynamic_slice_in_dim(value, me * length, length, 0)
    for shift in range(1, peers):
        other = lax.rem(me + shift, peers)
        part = lax.dynamic_slice_in_dim(value, other * length, length, 0)
        pairs = [(i, (i + shift) % peers) for i in range(peers)]
        total = total + lax.ppermute(part, "mem", pairs)
    return total


def collect(value):
    peers = lax.axis_size("mem")
    me = lax.axis_index("mem")
    length = value.shape[0]
    result = jnp.zeros((peers * length,) + value.shape[1:], value.dtype)
    result = lax.dynamic_update_slice_in_dim(result, value, me * length, 0)
    for shift in range(1, peers):
        pairs = [(i, (i + shift) % peers) for i in range(peers)]
        moved = lax.ppermute(value, "mem", pairs)
        source = lax.rem(me + peers - shift, peers)
        result = lax.dynamic_update_slice_in_dim(result, moved, source * length, 0)
    return result


def row_matrix(row_weights, fine_rows, coarse_rows):
    fine_index = lax.broadcasted_iota(jnp.int32, (fine_rows, coarse_rows), 0)
    coarse_index = lax.broadcasted_iota(jnp.int32, (fine_rows, coarse_rows), 1)
    weights = row_weights.astype(jnp.float32)
    stencil = jnp.zeros((fine_rows, coarse_rows), jnp.float32)
    for offset in range(3):
        matched = coarse_index == fine_index // 2 + offset - 1
        stencil = stencil + jnp.where(matched, weights[offset][:, None], 0.0)
    return stencil.astype(jnp.bfloat16)


def solve_weights(gram_sums, right_side):
    member_count = gram_sums.shape[-1]
    system = gram_sums + (member_count - 1) * jnp.eye(member_count, dtype=jnp.float32)
    factor = jnp.linalg.cholesky(system)
    halfway = lax.linalg.triangular_solve(factor, right_side[..., None], left_side=True, lower=True)
    result = lax.linalg.triangular_solve(
        factor, halfway, left_side=True, lower=True, transpose_a=True
    )
    return result[..., 0]


def plain_increment(
    ens_coarse, col_interp, row_weights, ctrl_vec, band_loc, row_loc, level_loc, total_members
):
    fine_rows = row_weights.shape[1]
    columns = band_loc.shape[0]
    coarse_cols = jnp.einsum(
        "tklic,jc->tklij", ens_coarse, col_interp, preferred_element_type=jnp.float32
    ).astype(jnp.bfloat16)
    stencil = row_matrix(row_weights, fine_rows, fine_rows // 2)
    refined = jnp.einsum(
        "tklij,ri->tkljr",
        lax.all_to_all(coarse_cols, "tile", split_axis=4, concat_axis=3, tiled=True),
        stencil,
        preferred_element_type=jnp.float32,
    ).astype(jnp.bfloat16)
    member_fine = refined[0]
    slot_term = member_fine * ctrl_vec[0][None]
    projected = slot_term.astype(jnp.bfloat16)
    if lax.axis_size("grp") > 1:
        projected = lax.psum(projected, "grp")
    padded = extended(projected, (("tile", 2),), columns)
    banded = jnp.einsum(
        "jq,klqr->kljr", band_loc, padded, preferred_element_type=jnp.float32
    ).astype(jnp.bfloat16)
    row_mixed = jnp.einsum(
        "kljs,rs->kljr", banded, row_loc, preferred_element_type=jnp.float32
    ).astype(jnp.bfloat16)
    localized = jnp.einsum(
        "lm,kmjr->kljr", level_loc, row_mixed, preferred_element_type=jnp.float32
    ).astype(jnp.bfloat16)
    return swap_add(
        jnp.sum(member_fine.astype(jnp.float32) * localized.astype(jnp.float32), axis=0)
    ) / (total_members - 1)


def member_kernel(
    before, own, after, ctrl, stencil, band, row_loc, level_loc, total, proj, fine, banded, mixed
):
    columns, levels, rows = total.shape
    window = proj.shape[0]

    @pl.when(pl.program_id(0) == 0)
    def _():
        total[...] = jnp.zeros_like(total)

    for q in range(window):
        source = (before, own, after)[q // columns]
        refined = lax.dot_general(
            source[0, q % columns],
            stencil[...],
            (((0,), (0,)), ((), ())),
            preferred_element_type=jnp.float32,
        ).astype(jnp.bfloat16)
        if q // columns == 1:
            fine[q % columns] = refined
        proj[q] = (refined.astype(jnp.float32) * ctrl[q]).astype(jnp.bfloat16)
    for pair in range(levels // (2 * GROUP)):
        parts = []
        for half in range(2):
            start = (2 * pair + half) * GROUP
            parts.append(proj[:, start : start + GROUP, :].reshape(window * GROUP, rows))
        result = jnp.dot(
            band[...], jnp.concatenate(parts, axis=1), preferred_element_type=jnp.float32
        ).astype(jnp.bfloat16)
        for half in range(2):
            start = (2 * pair + half) * GROUP
            banded[:, start : start + GROUP, :] = result[:, half * rows : (half + 1) * rows].reshape(
                columns, GROUP, rows
            )
    mixed[...] = lax.dot_general(
        banded[...].reshape(columns * levels, rows),
        row_loc[...],
        (((1,), (1,)), ((), ())),
        preferred_element_type=jnp.float32,
    ).astype(jnp.bfloat16)
    for j in range(columns):
        localized = jnp.dot(
            level_loc[...],
            mixed[j * levels : (j + 1) * levels, :],
            preferred_element_type=jnp.float32,
        )
        total[j] += fine[j].astype(jnp.float32) * localized


def member_sum(before, own, after, ctrl, stencil, band, row_loc, level_loc):
    members, columns, coarse_rows, levels = own.shape
    window, _, rows = ctrl.shape
    block = pl.BlockSpec((1, columns, coarse_rows, levels), lambda k: (k, 0, 0, 0))

    def whole(value):
        return pl.BlockSpec(value.shape, lambda k: (0,) * value.ndim)

    flops = 2 * members * levels * rows * (
        window * coarse_rows + columns * (window * GROUP + rows + levels)
    )
    return pl.pallas_call(
        member_kernel,
        grid=(members,),
        out_shape=jax.ShapeDtypeStruct((columns, levels, rows), jnp.float32),
        in_specs=[block, block, block]
        + [whole(value) for value in (ctrl, stencil, band, row_loc, level_loc)],
        out_specs=pl.BlockSpec((columns, levels, rows), lambda k: (0, 0, 0)),
        scratch_shapes=[
            pltpu.VMEM((window, levels, rows), jnp.bfloat16),
            pltpu.VMEM((columns, levels, rows), jnp.bfloat16),
            pltpu.VMEM((columns, levels, rows), jnp.bfloat16),
            pltpu.VMEM((columns * levels, rows), jnp.bfloat16),
        ],
        compiler_params=pltpu.CompilerParams(
            dimension_semantics=("arbitrary",), vmem_limit_bytes=24 * 1024 * 1024
        ),
        cost_estimate=pl.CostEstimate(
            flops=4 * flops, bytes_accessed=6 * own.size, transcendentals=0
        ),
    )(before, own, after, ctrl, stencil, band, row_loc, level_loc)


def neighbours(value):
    peers = lax.axis_size("tile")
    up = [(i, (i + 1) % peers) for i in range(peers - 1)]
    down = [(j, i) for i, j in up]
    return lax.ppermute(value, "tile", up), lax.ppermute(value, "tile", down)


def fused_increment(
    ens_coarse, col_interp, row_weights, ctrl_vec, band_loc, row_loc, level_loc, total_members
):
    fine_rows = row_weights.shape[1]
    stencil = row_matrix(row_weights, fine_rows, fine_rows // 2).T
    band = jnp.kron(band_loc, jnp.eye(GROUP, dtype=jnp.bfloat16))
    ctrl_own = jnp.swapaxes(ctrl_vec[0], 0, 1)
    ctrl_before, ctrl_after = neighbours(ctrl_own)
    ctrl = jnp.concatenate([ctrl_before, ctrl_own, ctrl_after], axis=0)
    members = ens_coarse.shape[1]
    chunks = CHUNKS if members % CHUNKS == 0 else 1
    size = members // chunks
    total = None
    for chunk in range(chunks):
        piece = ens_coarse[0, chunk * size : (chunk + 1) * size]
        coarse_cols = jnp.einsum(
            "klic,jc->jkil", piece, col_interp, preferred_element_type=jnp.float32
        ).astype(jnp.bfloat16)
        peers = lax.axis_size("tile")
        columns = coarse_cols.shape[0] // peers
        blocks = coarse_cols.reshape((peers, columns) + coarse_cols.shape[1:])
        moved = lax.all_to_all(blocks, "tile", split_axis=0, concat_axis=0, tiled=True)
        own = jnp.transpose(moved, (2, 1, 0, 3, 4))
        own = own.reshape(size, columns, -1, own.shape[-1])
        before, after = neighbours(own)
        part = member_sum(before, own, after, ctrl, stencil, band, row_loc, level_loc)
        total = part if total is None else total + part
    return swap_add(jnp.swapaxes(total, 0, 1)) / (total_members - 1)


def body(
    ens_coarse,
    col_interp,
    row_weights,
    ctrl_vec,
    band_loc,
    row_loc,
    level_loc,
    hx_pert,
    innov,
    obs_prec,
    obs_region,
):
    total_members = hx_pert.shape[1]
    observed = hx_pert[0]
    weighted = (observed * obs_prec[0][None, :]).astype(jnp.bfloat16)
    labels = lax.broadcasted_iota(jnp.int32, (NREG, observed.shape[1]), 0)
    member_of = obs_region[0][None, :] == labels
    masked = jnp.where(member_of[:, None, :], weighted[None], jnp.zeros((), jnp.bfloat16))
    gram_sums = jnp.einsum("rko,jo->rkj", masked, observed, preferred_element_type=jnp.float32)
    innov_rows = jnp.where(member_of, innov[0][None, :], 0.0)
    right_side = jnp.dot(
        innov_rows, weighted.astype(jnp.float32).T, precision=lax.Precision.HIGHEST
    )
    sums = jnp.concatenate([gram_sums, right_side[:, :, None]], axis=2)
    sums = swap_add(lax.psum(sums, "grp") if lax.axis_size("grp") > 1 else sums)
    plan = fused_increment if lax.axis_size("grp") == 1 else plain_increment
    increment = plan(
        ens_coarse, col_interp, row_weights, ctrl_vec, band_loc, row_loc, level_loc, total_members
    )
    own_weights = solve_weights(sums[:, :, :total_members], sums[:, :, total_members])
    weights = collect(own_weights)
    return (increment[None], weights)


def solution(mesh):
    placed = (
        P("grp", "mem", None, "tile", None),
        P(),
        P(),
        P("grp", None, "tile", None),
        P("tile", None),
        P(),
        P(),
        P("grp", None, ("tile", "mem")),
        P("grp", ("tile", "mem")),
        P("grp", ("tile", "mem")),
        P("grp", ("tile", "mem")),
    )
    return jax.shard_map(
        body,
        mesh=mesh,
        in_specs=placed,
        out_specs=(P("grp", "mem", "tile", None), P("tile", None)),
        check_vma=False,
    )
```

profile of v0, /device:TPU:9, one launch (start us, length us, event | category | flops | bytes accessed | tf_op | source)
XLA Modules:
  0.0 295.2 jit_solution(7241379773903900391)
XLA Ops:
  0.6 0.0 copy-start
  0.6 0.7 copy-done
  1.4 2.2 convert_bitcast_fusion
  3.5 4.9 %copy.39 = bf16[16,8,20,4,128]{4,3,1,2,0:T(4,128)(2,1)} copy(bf16[16,8,20,4,128]{4,1,0,3,2:T(8,128)(2,1)S(1)} %convert_bitcast_fusion) | data formatting | bytes 5242880 | tf_op jit(solution)/shard_map/reshape | solution.py:219
  8.5 6.5 %all-to-all-start.1 = ((bf16[16,8,20,4,128]{4,3,1,2,0:T(4,128)(2,1)}), bf16[16,8,20,4,128]{4,3,1,2,0:T(4,128)(2,1)S(1)}, u32[]{:S(2)}, u32[]{:S(2)}) async-start(bf16[16,8,20,4,128]{4,3,1,2,0:T(4,128)(2,1)} %copy.39), calls=%async_computation.1 | async-start | bytes 5242880 | tf_op jit(solution)/shard_map/all_to_all | solution.py:220
  15.0 2.2 convert_bitcast_fusion.1
  17.2 4.9 %copy.36 = bf16[16,8,20,4,128]{4,3,1,2,0:T(4,128)(2,1)} copy(bf16[16,8,20,4,128]{4,1,0,3,2:T(8,128)(2,1)S(1)} %convert_bitcast_fusion.1) | data formatting | bytes 5242880 | tf_op jit(solution)/shard_map/reshape | solution.py:219
  22.1 49.6 %all-to-all-done.1 = bf16[16,8,20,4,128]{4,3,1,2,0:T(4,128)(2,1)S(1)} async-done(((bf16[16,8,20,4,128]{4,3,1,2,0:T(4,128)(2,1)}), bf16[16,8,20,4,128]{4,3,1,2,0:T(4,128)(2,1)S(1)}, u32[]{:S(2)}, u32[]{:S(2)}) %all-to-all-start.1) | async-done | bytes 2621472 | tf_op jit(solution)/shard_map/all_to_all | solution.py:220
  71.6 1.5 copy-done.3
  73.2 6.8 %all-to-all-start = ((bf16[16,8,20,4,128]{4,3,1,2,0:T(4,128)(2,1)}), bf16[16,8,20,4,128]{4,3,1,2,0:T(4,128)(2,1)}, u32[]{:S(2)}, u32[]{:S(2)}) async-start(bf16[16,8,20,4,128]{4,3,1,2,0:T(4,128)(2,1)} %copy.36), calls=%async_computation | async-start | bytes 5242880 | tf_op jit(solution)/shard_map/all_to_all | solution.py:220
  80.0 0.0 copy-done.7
  80.0 0.0 copy-done.8
  80.0 0.0 copy-done.9
  80.0 0.0 copy-done.13
  80.0 0.3 fusion.10
  80.4 0.1 fusion.9
  80.5 0.0 copy-start.5
  80.5 0.0 copy-start.12
  80.5 1.2 fusion
  81.7 0.7 copy-done.4
  82.4 0.7 fusion.16
  83.1 1.2 collective-permute-start.7
  84.4 0.0 copy-done.5
  84.4 0.9 copy.52
  85.2 3.6 %collective-permute-start.2 = (f32[8,128,128]{2,1,0:T(8,128)}, f32[8,128,128]{2,1,0:T(8,128)}, u32[]{:S(2)}, u32[]{:S(2)}) collective-permute-start(f32[8,128,128]{2,1,0:T(8,128)} %bitcast.85), channel_id=1, source_target_pairs={{0,2},{2,4},{4,6},{6,8},{8,10},{10,12},{12,14},{14,16},{16,18},{18... | collective-permute-start | bytes 1572872 | tf_op jit(solution)/shard_map/ppermute | solution.py:196
  88.9 0.7 copy.42
  89.6 0.0 copy-done.12
  89.6 0.0 copy-start.11
  89.6 3.2 %copy.40 = bf16[20,8,16,4,128]{4,3,2,1,0:T(4,128)(2,1)S(1)} copy(bf16[20,8,16,4,128]{4,3,1,0,2:T(4,128)(2,1)} %bitcast.89) | data formatting | bytes 5242880 | tf_op jit(solution)/shard_map/transpose | solution.py:221
  92.9 1.9 collective-permute-start.4
  94.8 2.6 collective-permute-start.5
  97.4 0.1 broadcast_multiply_fusion
  97.5 0.5 mul.62.band
  98.2 0.0 collective-permute-done.7
  98.2 1.0 fusion.18
  99.2 0.8 slice_add_fusion
  100.0 0.1 copy.43
  100.1 39.6 %all-to-all-done = bf16[16,8,20,4,128]{4,3,1,2,0:T(4,128)(2,1)} async-done(((bf16[16,8,20,4,128]{4,3,1,2,0:T(4,128)(2,1)}), bf16[16,8,20,4,128]{4,3,1,2,0:T(4,128)(2,1)}, u32[]{:S(2)}, u32[]{:S(2)}) %all-to-all-start) | async-done | bytes 2621472 | tf_op jit(solution)/shard_map/all_to_all | solution.py:220
  139.7 4.7 %copy.37 = bf16[20,8,16,4,128]{4,3,2,1,0:T(4,128)(2,1)} copy(bf16[20,8,16,4,128]{4,3,1,0,2:T(4,128)(2,1)} %bitcast.5) | data formatting | bytes 5242880 | tf_op jit(solution)/shard_map/transpose | solution.py:221
  144.4 4.3 %collective-permute-start = (bf16[20,8,64,128]{3,2,1,0:T(8,128)(2,1)}, bf16[20,8,64,128]{3,2,1,0:T(8,128)(2,1)}, u32[]{:S(2)}, u32[]{:S(2)}) collective-permute-start(bf16[20,8,64,128]{3,2,1,0:T(8,128)(2,1)} %bitcast.6.own), channel_id=1, source_target_pairs={{0,2},{2,4},{4,6},{6,8},{8,10},{10,12},{12,14},{14,16},{16,18},{18... | collective-permute-start | bytes 7864328 | tf_op jit(solution)/shard_map/ppermute | solution.py:196
  148.7 1.9 collective-permute-start.1
  150.6 0.0 copy-done.6
  150.7 29.3 %custom-call.9 = f32[4,80,80]{2,1,0:T(8,128)S(1)} custom-call(f32[4,80,80]{2,1,0:T(8,128)S(1)} %fusion.22), custom_call_target="Cholesky" | custom-call | tf_op jit(solution)/shard_map/jit(cholesky)/cholesky | solution.py:67
  180.0 0.0 collective-permute-done.2
  180.0 2.1 collective-permute-start.3
  182.1 0.1 compare_reduce_fusion
  182.2 0.1 select_bitcast_fusion
  182.3 24.6 %custom-call.10 = f32[4,1,80,80]{2,3,1,0:T(8,128)S(1)} custom-call(f32[4,1,80,80]{3,2,1,0:T(8,128)S(1)} %select_bitcast_fusion), custom_call_target="InvertDiagBlocksLowerTriangular" | custom-call | tf_op jit(solution)/shard_map/triangular_solve | solution.py:69
  206.9 0.3 convolution_bitcast_fusion
  207.2 33.6 %collective-permute-done.3 = f32[8,128,128]{2,1,0:T(8,128)} collective-permute-done((f32[8,128,128]{2,1,0:T(8,128)}, f32[8,128,128]{2,1,0:T(8,128)}, u32[]{:S(2)}, u32[]{:S(2)}) %collective-permute-start.3) | collective-permute-done | bytes 524320 | tf_op jit(solution)/shard_map/ppermute | solution.py:196
  240.8 1.5 pad_maximum_fusion.ctrl
  242.3 0.0 collective-permute-done.4.before
  242.3 0.0 collective-permute-done.5.after
  242.3 23.2 %shard_map.123 = f32[8,128,128]{2,1,0:T(8,128)S(1)} custom-call(bf16[20,8,64,128]{3,2,1,0:T(8,128)(2,1)} %collective-permute-done.4.before, bf16[20,8,64,128]{3,2,1,0:T(8,128)(2,1)S(1)} %bitcast.88, bf16[20,8,64,128]{3,2,1,0:T(8,128)(2,1)} %collective-permute-done.5.after, f32[24,128,128]{2,1,0:T(8,128)S(1)} %pad_maximum_fusion.ctrl, ...), custom_call_target="tpu_custom_call" | custom-call | flops 17448304640 | bytes 7864320 | tf_op jit(solution)/shard_map/pallas_call | solution.py:170
  265.5 0.0 collective-permute-done.before
  265.5 0.0 collective-permute-done.1.after
  265.5 23.3 %shard_map.122 = f32[8,128,128]{2,1,0:T(8,128)S(1)} custom-call(bf16[20,8,64,128]{3,2,1,0:T(8,128)(2,1)} %collective-permute-done.before, bf16[20,8,64,128]{3,2,1,0:T(8,128)(2,1)} %bitcast.6.own, bf16[20,8,64,128]{3,2,1,0:T(8,128)(2,1)} %collective-permute-done.1.after, f32[24,128,128]{2,1,0:T(8,128)S(1)} %pad_maximum_fusion.ctrl, ...), custom_call_target="tpu_custom_call" | custom-call | flops 17448304640 | bytes 7864320 | tf_op jit(solution)/shard_map/pallas_call | solution.py:170
  288.8 0.1 add.79
  288.9 0.5 collective-permute-start.6
  289.4 0.4 fusion.19
  289.8 1.1 collective-permute-start.8
  290.8 3.4 %collective-permute-done.8 = f32[4,80]{1,0:T(4,128)S(1)} collective-permute-done((f32[4,80]{1,0:T(4,128)S(1)}, f32[4,80]{1,0:T(4,128)S(1)}, u32[]{:S(2)}, u32[]{:S(2)}) %collective-permute-start.8) | collective-permute-done | bytes 1312 | tf_op jit(solution)/shard_map/ppermute | solution.py:47
  294.2 0.0 collective-permute-done.6
  294.3 0.9 copy.44
  (31 shorter events, 0.3 us)
Async XLA Ops:
  0.6 0.7 copy-start
  8.5 63.2 %all-to-all-start.1 = ((bf16[16,8,20,4,128]{4,3,1,2,0:T(4,128)(2,1)}), bf16[16,8,20,4,128]{4,3,1,2,0:T(4,128)(2,1)S(1)}, u32[]{:S(2)}, u32[]{:S(2)}) async-start(bf16[16,8,20,4,128]{4,3,1,2,0:T(4,128)(2,1)} %copy.39), calls=%async_computation.1 | async-start | bytes 5242880 | tf_op jit(solution)/shard_map/all_to_all | solution.py:220
  22.1 57.9 %copy-start.7 = (bf16[1,80,2048]{2,1,0:T(8,128)(2,1)S(1)}, bf16[1,80,2048]{2,1,0:T(8,128)(2,1)}, u32[]{:S(2)}) copy-start(bf16[1,80,2048]{2,1,0:T(8,128)(2,1)} %param.18) | copy-start | bytes 983044
  22.1 57.9 %copy-start.8 = (s32[1,2048]{1,0:T(1,128)S(1)}, s32[1,2048]{1,0:T(1,128)}, u32[]{:S(2)}) copy-start(s32[1,2048]{1,0:T(1,128)} %param.21) | copy-start | bytes 24580
  22.1 57.9 %copy-start.9 = (f32[1,2048]{1,0:T(1,128)S(1)}, f32[1,2048]{1,0:T(1,128)}, u32[]{:S(2)}) copy-start(f32[1,2048]{1,0:T(1,128)} %param.20) | copy-start | bytes 24580
  22.1 57.9 %copy-start.13 = (f32[1,2048]{1,0:T(1,128)S(1)}, f32[1,2048]{1,0:T(1,128)}, u32[]{:S(2)}) copy-start(f32[1,2048]{1,0:T(1,128)} %param.19) | copy-start | bytes 24580
  71.6 1.5 copy-start.3
  73.2 66.5 %all-to-all-start = ((bf16[16,8,20,4,128]{4,3,1,2,0:T(4,128)(2,1)}), bf16[16,8,20,4,128]{4,3,1,2,0:T(4,128)(2,1)}, u32[]{:S(2)}, u32[]{:S(2)}) async-start(bf16[16,8,20,4,128]{4,3,1,2,0:T(4,128)(2,1)} %copy.36), calls=%async_computation | async-start | bytes 5242880 | tf_op jit(solution)/shard_map/all_to_all | solution.py:220
  80.5 3.9 %copy-start.5 = (f32[1,128,8,128]{3,2,1,0:T(8,128)S(1)}, f32[1,128,8,128]{3,2,1,0:T(8,128)}, u32[]{:S(2)}) copy-start(f32[1,128,8,128]{3,2,1,0:T(8,128)} %param.14) | copy-start | bytes 1572868
  80.5 9.1 %copy-start.12 = (bf16[3,128]{1,0:T(4,128)(2,1)S(1)}, bf16[3,128]{1,0:T(4,128)(2,1)}, u32[]{:S(2)}) copy-start(bf16[3,128]{1,0:T(4,128)(2,1)} %param.13) | copy-start | bytes 2308
  81.7 0.7 copy-start.4
  83.1 15.0 %collective-permute-start.7 = (f32[4,80,81]{1,2,0:T(8,128)}, f32[4,80,81]{1,2,0:T(8,128)}, u32[]{:S(2)}, u32[]{:S(2)}) collective-permute-start(f32[4,80,81]{1,2,0:T(8,128)} %fusion.16), channel_id=1, source_target_pairs={{0,1},{1,0},{2,3},{3,2},{4,5},{5,4},{6,7},{7,6},{8,9},{9,8},{10,11... | collective-permute-start | bytes 311048 | tf_op jit(solution)/shard_map/ppermute | solution.py:35
  85.2 94.8 %collective-permute-start.2 = (f32[8,128,128]{2,1,0:T(8,128)}, f32[8,128,128]{2,1,0:T(8,128)}, u32[]{:S(2)}, u32[]{:S(2)}) collective-permute-start(f32[8,128,128]{2,1,0:T(8,128)} %bitcast.85), channel_id=1, source_target_pairs={{0,2},{2,4},{4,6},{6,8},{8,10},{10,12},{12,14},{14,16},{16,18},{18... | collective-permute-start | bytes 1572872 | tf_op jit(solution)/shard_map/ppermute | solution.py:196
  89.6 7.8 %copy-start.11 = (bf16[8,24]{1,0:T(8,128)(2,1)S(1)}, bf16[8,24]{1,0:T(8,128)(2,1)}, u32[]{:S(2)}) copy-start(bf16[8,24]{1,0:T(8,128)(2,1)} %param.15) | copy-start | bytes 1156
  92.9 149.4 %collective-permute-start.4 = (bf16[20,8,64,128]{3,2,1,0:T(8,128)(2,1)S(1)}, bf16[20,8,64,128]{3,2,1,0:T(8,128)(2,1)}, u32[]{:S(2)}, u32[]{:S(2)}) collective-permute-start(bf16[20,8,64,128]{3,2,1,0:T(8,128)(2,1)S(1)} %bitcast.86), channel_id=1, source_target_pairs={{0,2},{2,4},{4,6},{6,8},{8,10},{10,12},{12,14},{14,16},{16,18},{18... | collective-permute-start | bytes 7864328 | tf_op jit(solution)/shard_map/ppermute | solution.py:196
  94.8 147.5 %collective-permute-start.5 = (bf16[20,8,64,128]{3,2,1,0:T(8,128)(2,1)S(1)}, bf16[20,8,64,128]{3,2,1,0:T(8,128)(2,1)}, u32[]{:S(2)}, u32[]{:S(2)}) collective-permute-start(bf16[20,8,64,128]{3,2,1,0:T(8,128)(2,1)S(1)} %bitcast.87), channel_id=1, source_target_pairs={{2,0},{4,2},{6,4},{8,6},{10,8},{12,10},{14,12},{16,14},{18,16},{20... | collective-permute-start | bytes 7864328 | tf_op jit(solution)/shard_map/ppermute | solution.py:196
  139.7 10.9 %copy-start.6 = (f32[80,80]{0,1:T(8,128)S(1)}, f32[80,80]{0,1:T(8,128)}, u32[]{:S(2)}) copy-start(f32[80,80]{0,1:T(8,128)} %copy.42) | copy-start | bytes 76804
  144.4 97.9 %copy-start.1 = (bf16[128,128]{1,0:T(8,128)(2,1)S(1)}, bf16[128,128]{1,0:T(8,128)(2,1)}, u32[]{:S(2)}) copy-start(bf16[128,128]{1,0:T(8,128)(2,1)} %row_loc.3) | copy-start | bytes 98308
  144.4 97.9 %copy-start.2 = (bf16[128,128]{1,0:T(8,128)(2,1)S(1)}, bf16[128,128]{1,0:T(8,128)(2,1)}, u32[]{:S(2)}) copy-start(bf16[128,128]{1,0:T(8,128)(2,1)} %level_loc.3) | copy-start | bytes 98308
  144.4 121.1 %collective-permute-start = (bf16[20,8,64,128]{3,2,1,0:T(8,128)(2,1)}, bf16[20,8,64,128]{3,2,1,0:T(8,128)(2,1)}, u32[]{:S(2)}, u32[]{:S(2)}) collective-permute-start(bf16[20,8,64,128]{3,2,1,0:T(8,128)(2,1)} %bitcast.6.own), channel_id=1, source_target_pairs={{0,2},{2,4},{4,6},{6,8},{8,10},{10,12},{12,14},{14,16},{16,18},{18... | collective-permute-start | bytes 7864328 | tf_op jit(solution)/shard_map/ppermute | solution.py:196
  148.7 116.8 %collective-permute-start.1 = (bf16[20,8,64,128]{3,2,1,0:T(8,128)(2,1)}, bf16[20,8,64,128]{3,2,1,0:T(8,128)(2,1)}, u32[]{:S(2)}, u32[]{:S(2)}) collective-permute-start(bf16[20,8,64,128]{3,2,1,0:T(8,128)(2,1)} %bitcast.6.own), channel_id=1, source_target_pairs={{2,0},{4,2},{6,4},{8,6},{10,8},{12,10},{14,12},{16,14},{18,16},{20... | collective-permute-start | bytes 7864328 | tf_op jit(solution)/shard_map/ppermute | solution.py:196
  180.0 60.8 %collective-permute-start.3 = (f32[8,128,128]{2,1,0:T(8,128)}, f32[8,128,128]{2,1,0:T(8,128)}, u32[]{:S(2)}, u32[]{:S(2)}) collective-permute-start(f32[8,128,128]{2,1,0:T(8,128)} %bitcast.85), channel_id=1, source_target_pairs={{2,0},{4,2},{6,4},{8,6},{10,8},{12,10},{14,12},{16,14},{18,16},{20... | collective-permute-start | bytes 1572872 | tf_op jit(solution)/shard_map/ppermute | solution.py:196
  288.9 5.3 %collective-permute-start.6 = (f32[64,8,128]{2,0,1:T(8,128)S(1)}, f32[64,8,128]{2,0,1:T(8,128)S(1)}, u32[]{:S(2)}, u32[]{:S(2)}) collective-permute-start(f32[64,8,128]{2,0,1:T(8,128)S(1)} %dynamic-slice_bitcast_fusion), channel_id=1, source_target_pairs={{0,1},{1,0},{2,3},{3,2},{4,5},{5,4},{6,7},{7,6},{8,9},{9,8},{10,11... | collective-permute-start | bytes 786440 | tf_op jit(solution)/shard_map/ppermute | solution.py:35
  289.8 4.5 %collective-permute-start.8 = (f32[4,80]{1,0:T(4,128)S(1)}, f32[4,80]{1,0:T(4,128)S(1)}, u32[]{:S(2)}, u32[]{:S(2)}) collective-permute-start(f32[4,80]{1,0:T(4,128)S(1)} %bitcast.92), channel_id=1, source_target_pairs={{0,1},{1,0},{2,3},{3,2},{4,5},{5,4},{6,7},{7,6},{8,9},{9,8},{10,11... | collective-permute-start | bytes 3848 | tf_op jit(solution)/shard_map/ppermute | solution.py:47
  294.2 0.9 copy-start.10
where the time goes:
time: 296 us; the launch traced here: 295 us
  waiting for transfers between devices  126 us (43%)
  other arithmetic  58.6 us (20%)
  Pallas kernels  46.5 us (16%)
  starting transfers between devices  32.6 us (11%)
  local copies, waits for them, and re-layouts  23.9 us (8%)
  matrix products  6.53 us (2%)
    all_to_all x2, waiting for transfers between devices, fused_increment(): lax.all_to_all(blocks, 'tile', split_axis=0, concat_axis=0, tiled=True)  89.1 us
    pallas_call x2, Pallas kernels, member_sum(): pl.pallas_call(member_kernel, grid=(members,), out_shape=jax.ShapeDtypeSt...  46.5 us
    ppermute x6, waiting for transfers between devices, neighbours(): return (lax.ppermute(value, 'tile', up), lax.ppermute(value, 'tile', down))  33.6 us
    another operation x4, other arithmetic, solve_weights(): factor = jnp.linalg.cholesky(system)  29.5 us
    another operation x3, other arithmetic, solve_weights(): lax.linalg.triangular_solve(factor, halfway, left_side=True, lower=True,...  24.7 us
    ppermute x6, starting transfers between devices, neighbours(): return (lax.ppermute(value, 'tile', up), lax.ppermute(value, 'tile', down))  16.4 us
    all_to_all x2, starting transfers between devices, fused_increment(): lax.all_to_all(blocks, 'tile', split_axis=0, concat_axis=0, tiled=True)  13.4 us
    reshape x2, local copies, waits for them, and re-layouts, fused_increment(): blocks = coarse_cols.reshape((peers, columns) + coarse_cols.shape[1:])  9.78 us
  transfers between devices with their start and end apart: 11, of which 4 were waited for; matrix products, arithmetic and copies ran while one was open for 26% of the time, Pallas kernels for 8%

commit v1 on v0

--- a/solution.py
+++ b/solution.py
@@ -1,3 +1,5 @@
+import functools
+
 import jax
 import jax.numpy as jnp
 from jax import lax
@@ -7,7 +9,7 @@
 
 NREG = 8
 GROUP = 16
-CHUNKS = 2
+MESH = pl.DeviceIdType.MESH
 
 
 def extended(value, sides, width):
@@ -107,123 +109,421 @@
     ) / (total_members - 1)
 
 
-def member_kernel(
-    before, own, after, ctrl, stencil, band, row_loc, level_loc, total, proj, fine, banded, mixed
+def place():
+    tile = lax.axis_index("tile")
+    core = lax.rem(tile, 2)
+    chip = lax.div(tile, 2)
+    return lax.div(chip, 2), lax.rem(chip, 2), core, lax.axis_index("mem")
+
+
+def target(z, x, core, y):
+    return {"tile": (z * 2 + x) * 2 + core, "mem": y}
+
+
+def greet(peers):
+    barrier = pltpu.get_barrier_semaphore()
+    for peer in peers:
+        pl.semaphore_signal(barrier, inc=1, device_id=peer, device_id_type=MESH)
+    pl.semaphore_wait(barrier, len(peers))
+
+
+def spread_kernel(depth, own, slots, halo, send_a, recv_a, send_x, recv_x, send_y, recv_y, send_h, recv_h, local):
+    z, x, core, y = place()
+    per_side = 2 * depth // 4
+    side = lax.div(z, per_side)
+    line = [(lax.rem(z + dz, depth), lax.rem(core + dc, 2)) for dz in range(depth) for dc in range(2)]
+    greet(
+        [target(zz, x, cc, y) for zz, cc in line[1:]]
+        + [target(z, 1 - x, core, y), target(z, x, core, 1 - y)]
+    )
+    mine = lax.rem(z, per_side) * 4 + x * 2 + core
+    kind = lax.rem(z, per_side) * 2 + core
+    for zz in range(depth):
+        to_self = jnp.logical_and(z == zz, core == side)
+
+        @pl.when(jnp.logical_not(to_self))
+        def _():
+            pltpu.make_async_remote_copy(
+                own.at[y], slots.at[mine, y], send_a.at[zz], recv_a.at[kind],
+                target(zz, x, side, y), MESH,
+            ).start()
+
+        @pl.when(to_self)
+        def _():
+            pltpu.make_async_copy(own.at[y], slots.at[mine, y], recv_a.at[kind]).start()
+
+    def arrived(slot, half, sem):
+        pltpu.make_async_copy(slots.at[slot, half], slots.at[slot, half], sem).wait()
+
+    def forward(slot, half, send, recv, peer):
+        pltpu.make_async_remote_copy(
+            slots.at[slot, half], slots.at[slot, half], send, recv, peer, MESH
+        ).start()
+
+    count = per_side * 2
+    across, beside = target(z, x, core, 1 - y), target(z, 1 - x, core, y)
+    for k in range(count):
+        slot = (k // 2) * 4 + x * 2 + k % 2
+        arrived(slot, y, recv_a.at[k])
+        forward(slot, y, send_x.at[k], recv_x.at[k], beside)
+        forward(slot, y, send_y.at[k], recv_y.at[k], across)
+    for k in range(count):
+        slot = (k // 2) * 4 + (1 - x) * 2 + k % 2
+        arrived(slot, y, recv_x.at[k])
+        forward(slot, y, send_y.at[count + k], recv_y.at[count + k], across)
+    for k in range(count):
+        arrived((k // 2) * 4 + x * 2 + k % 2, 1 - y, recv_y.at[k])
+    for k in range(count):
+        arrived((k // 2) * 4 + (1 - x) * 2 + k % 2, 1 - y, recv_y.at[count + k])
+    edge = (1 - core) * (2 * count - 1)
+    last = pltpu.make_async_remote_copy(
+        slots.at[edge], halo, send_h, recv_h, target(z, x, 1 - core, y), MESH
+    )
+    last.start()
+    for k in range(count):
+        arrived((k // 2) * 4 + x * 2 + k % 2, y, send_x.at[k])
+    for k in range(2 * count):
+        arrived(k, y, send_y.at[k])
+    for zz in range(depth):
+        @pl.when(jnp.logical_not(jnp.logical_and(z == zz, core == side)))
+        def _():
+            pltpu.make_async_copy(own.at[y], own.at[y], send_a.at[zz]).wait()
+    last.wait()
+
+
+def spread(own, depth):
+    shape = (depth * 2,) + own.shape
+    dma = pltpu.SemaphoreType.DMA
+    count = depth
+    return pl.pallas_call(
+        functools.partial(spread_kernel, depth),
+        out_shape=(
+            jax.ShapeDtypeStruct(shape, own.dtype),
+            jax.ShapeDtypeStruct(own.shape, own.dtype),
+        ),
+        in_specs=[pl.BlockSpec(memory_space=pltpu.VMEM)],
+        out_specs=(pl.BlockSpec(memory_space=pl.ANY),) * 2,
+        scratch_shapes=[
+            dma((depth,)), dma((count,)), dma((count,)), dma((count,)),
+            dma((2 * count,)), dma((2 * count,)), dma, dma, dma,
+        ],
+        compiler_params=pltpu.CompilerParams(collective_id=0, has_side_effects=True),
+        cost_estimate=pl.CostEstimate(flops=10**9, bytes_accessed=10**7, transcendentals=0),
+    )(own)
+
+
+def ensemble_kernel(
+    first, own, other, slots, halo, interp, stencil, row_loc, level_loc, start, total,
+    coarse, fine, proj, banded, kron, acc
 ):
-    columns, levels, rows = total.shape
-    window = proj.shape[0]
-
-    @pl.when(pl.program_id(0) == 0)
+    member = pl.program_id(0)
+    sources = own.shape[0]
+    columns, rows, levels = fine.shape
+    coarse_rows = stencil.shape[1]
+    kept = acc.shape[0]
+    stride = coarse_rows + 8
+    core = lax.rem(lax.axis_index("tile"), 2)
+    f32 = jnp.float32
+
+    @pl.when(member == 0)
     def _():
-        total[...] = jnp.zeros_like(total)
-
-    for q in range(window):
-        source = (before, own, after)[q // columns]
-        refined = lax.dot_general(
-            source[0, q % columns],
-            stencil[...],
-            (((0,), (0,)), ((), ())),
-            preferred_element_type=jnp.float32,
+        if first:
+            acc[...] = jnp.zeros_like(acc)
+        else:
+            acc[...] = start[...].astype(f32)
+        spread_rows = (
+            lax.broadcasted_iota(jnp.int32, (128, 8), 0) // GROUP
+            == lax.broadcasted_iota(jnp.int32, (128, 8), 1)
         ).astype(jnp.bfloat16)
-        if q // columns == 1:
-            fine[q % columns] = refined
-        proj[q] = (refined.astype(jnp.float32) * ctrl[q]).astype(jnp.bfloat16)
-    for pair in range(levels // (2 * GROUP)):
-        parts = []
-        for half in range(2):
-            start = (2 * pair + half) * GROUP
-            parts.append(proj[:, start : start + GROUP, :].reshape(window * GROUP, rows))
-        result = jnp.dot(
-            band[...], jnp.concatenate(parts, axis=1), preferred_element_type=jnp.float32
+        spread_cols = (
+            lax.broadcasted_iota(jnp.int32, (128, 24 * GROUP), 0)
+            == lax.broadcasted_iota(jnp.int32, (128, 24 * GROUP), 1) // GROUP
         ).astype(jnp.bfloat16)
-        for half in range(2):
-            start = (2 * pair + half) * GROUP
-            banded[:, start : start + GROUP, :] = result[:, half * rows : (half + 1) * rows].reshape(
-                columns, GROUP, rows
-            )
-    mixed[...] = lax.dot_general(
-        banded[...].reshape(columns * levels, rows),
-        row_loc[...],
-        (((1,), (1,)), ((), ())),
-        preferred_element_type=jnp.float32,
-    ).astype(jnp.bfloat16)
-    for j in range(columns):
-        localized = jnp.dot(
-            level_loc[...],
-            mixed[j * levels : (j + 1) * levels, :],
-            preferred_element_type=jnp.float32,
+        same = lax.rem(lax.broadcasted_iota(jnp.int32, (128, 24 * GROUP), 0), GROUP) == lax.rem(
+            lax.broadcasted_iota(jnp.int32, (128, 24 * GROUP), 1), GROUP
         )
-        total[j] += fine[j].astype(jnp.float32) * localized
-
-
-def member_sum(before, own, after, ctrl, stencil, band, row_loc, level_loc):
-    members, columns, coarse_rows, levels = own.shape
-    window, _, rows = ctrl.shape
-    block = pl.BlockSpec((1, columns, coarse_rows, levels), lambda k: (k, 0, 0, 0))
+        for b in range(kept // 8):
+            band = slots[b, 0, 4 * rows : 4 * rows + 8, :]
+            tall = jnp.dot(spread_rows, band, preferred_element_type=f32).astype(jnp.bfloat16)
+            wide = jnp.dot(tall, spread_cols, preferred_element_type=f32)
+            kron[b] = jnp.where(same, wide, 0.0).astype(jnp.bfloat16)
+
+    for source in range(sources):
+        for part in range(2):
+            held = (own, other)[part]
+            row = 4 * source + 2 * (core if part == 0 else 1 - core)
+            pair = jnp.concatenate([held[source, 0, 0], held[source, 0, 1]], axis=1)
+            mixed = jnp.dot(interp[...], pair, preferred_element_type=f32)
+            for k in range(2):
+                coarse[pl.ds(row + k, columns, stride=stride), :] = mixed[:, k * levels : (k + 1) * levels]
+
+    def refine(pair, table):
+        base = 2 * pair * stride
+        joined = jnp.concatenate(
+            [coarse[pl.ds(base + k * stride, coarse_rows), :].astype(jnp.bfloat16) for k in range(2)], axis=1
+        )
+        result = jnp.dot(stencil[...], joined, preferred_element_type=f32).astype(jnp.bfloat16)
+        for k in range(2):
+            piece = result[:, k * levels : (k + 1) * levels]
+            j = 2 * pair + k
+            fine[j] = piece
+            proj[j] = (piece.astype(f32) * table(k).astype(f32)).astype(jnp.bfloat16)
+
+    def edge(pair, column):
+        def table(k):
+            j = column + k
+            return halo[j // 4, (j % 4) * rows : (j % 4 + 1) * rows, :]
+        refine(pair, table)
+
+    for pair in range(4):
+        edge(pair, 2 * pair)
+        edge(columns // 2 - 4 + pair, 2 * pair)
+
+    @pl.loop(0, kept // 8)
+    def _(b):
+        for pair in range(4):
+            def table(k):
+                j = 2 * pair + k
+                return slots[b, j // 4, (j % 4) * rows : (j % 4 + 1) * rows, :]
+            refine(4 + 4 * b + pair, table)
+
+    @pl.loop(0, kept // 8)
+    def _(b):
+        for pair in range(rows // (2 * GROUP)):
+            parts = []
+            for k in range(2):
+                at = (2 * pair + k) * GROUP
+                parts.append(proj[pl.ds(8 * b, 24), at : at + GROUP, :].reshape(24 * GROUP, levels))
+            result = jnp.dot(
+                kron[b], jnp.concatenate(parts, axis=1), preferred_element_type=f32
+            ).astype(jnp.bfloat16)
+            for k in range(2):
+                at = (2 * pair + k) * GROUP
+                banded[:, at : at + GROUP, :] = result[:, k * levels : (k + 1) * levels].reshape(
+                    8, GROUP, levels
+                )
+        for pair in range(4):
+            joined = jnp.concatenate([banded[2 * pair], banded[2 * pair + 1]], axis=1)
+            mixed = jnp.dot(row_loc[...], joined, preferred_element_type=f32).astype(jnp.bfloat16)
+            localized = jnp.dot(mixed, level_loc[...], preferred_element_type=f32)
+            for k in range(2):
+                j = 8 * b + 2 * pair + k
+                acc[j] += fine[8 + j].astype(f32) * localized[:, k * levels : (k + 1) * levels]
+
+    @pl.when(member == pl.num_programs(0) - 1)
+    def _():
+        total[...] = acc[...].astype(total.dtype)
+
+
+def ensemble_sum(own, other, slots, halo, interp, stencil, row_loc, level_loc, start):
+    sources, members, _, width, levels = own.shape
+    columns = interp.shape[0]
+    rows, coarse_rows = stencil.shape
+    kept = columns - 16
+    first = start is None
+    shape = (kept, rows, levels)
+    if first:
+        start = jnp.zeros((8, 128), jnp.float32)
+    block = pl.BlockSpec((sources, 1, 2, width, levels), lambda k: (0, k, 0, 0, 0))
 
     def whole(value):
         return pl.BlockSpec(value.shape, lambda k: (0,) * value.ndim)
 
-    flops = 2 * members * levels * rows * (
-        window * coarse_rows + columns * (window * GROUP + rows + levels)
-    )
+    constants = (slots, halo, interp, stencil, row_loc, level_loc, start)
+    flops = 2 * members * levels * rows * columns * (coarse_rows + 24 * GROUP + rows + levels)
+    bf16 = jnp.bfloat16
     return pl.pallas_call(
-        member_kernel,
+        functools.partial(ensemble_kernel, first),
         grid=(members,),
-        out_shape=jax.ShapeDtypeStruct((columns, levels, rows), jnp.float32),
-        in_specs=[block, block, block]
-        + [whole(value) for value in (ctrl, stencil, band, row_loc, level_loc)],
-        out_specs=pl.BlockSpec((columns, levels, rows), lambda k: (0, 0, 0)),
+        out_shape=jax.ShapeDtypeStruct(shape, jnp.bfloat16),
+        in_specs=[block, block] + [whole(value) for value in constants],
+        out_specs=pl.BlockSpec(shape, lambda k: (0, 0, 0)),
         scratch_shapes=[
-            pltpu.VMEM((window, levels, rows), jnp.bfloat16),
-            pltpu.VMEM((columns, levels, rows), jnp.bfloat16),
-            pltpu.VMEM((columns, levels, rows), jnp.bfloat16),
-            pltpu.VMEM((columns * levels, rows), jnp.bfloat16),
+            pltpu.VMEM((columns * (coarse_rows + 8), levels), jnp.float32),
+            pltpu.VMEM((columns, rows, levels), bf16),
+            pltpu.VMEM((columns, rows, levels), bf16),
+            pltpu.VMEM((8, rows, levels), bf16),
+            pltpu.VMEM((kept // 8, 8 * GROUP, 24 * GROUP), bf16),
+            pltpu.VMEM(shape, jnp.float32),
         ],
         compiler_params=pltpu.CompilerParams(
-            dimension_semantics=("arbitrary",), vmem_limit_bytes=24 * 1024 * 1024
+            dimension_semantics=("arbitrary",), vmem_limit_bytes=40 * 1024 * 1024
         ),
-        cost_estimate=pl.CostEstimate(
-            flops=4 * flops, bytes_accessed=6 * own.size, transcendentals=0
-        ),
-    )(before, own, after, ctrl, stencil, band, row_loc, level_loc)
-
-
-def neighbours(value):
-    peers = lax.axis_size("tile")
-    up = [(i, (i + 1) % peers) for i in range(peers - 1)]
-    down = [(j, i) for i, j in up]
-    return lax.ppermute(value, "tile", up), lax.ppermute(value, "tile", down)
-
-
-def fused_increment(
+        cost_estimate=pl.CostEstimate(flops=flops, bytes_accessed=4 * own.size, transcendentals=0),
+    )(own, other, *constants)
+
+
+def gather_kernel(
+    depth, scale, part, result, near, sums, far, turned, swap_out, swap_in,
+    send_near, recv_near, send_far, recv_far, send_y, recv_y
+):
+    z, x, core, y = place()
+    per_side = depth // 2
+    side = lax.div(z, per_side)
+    columns, rows = part.shape[1], part.shape[2]
+    half = rows // 2
+    line = [(lax.rem(z + dz, depth), lax.rem(core + dc, 2)) for dz in range(depth) for dc in range(2)]
+    partners = [(1 - x, y), (x, 1 - y), (1 - x, 1 - y)]
+    greet(
+        [target(zz, x, cc, y) for zz, cc in line[1:]]
+        + [target(z, xx, core, yy) for xx, yy in partners]
+    )
+    count = per_side * 2
+    f32 = jnp.float32
+
+    def rows_of(yy):
+        return pl.ds(pl.multiple_of(yy * half, half), half)
+
+    def near_copy(k, n):
+        xx, yy = partners[n]
+        return pltpu.make_async_remote_copy(
+            part.at[(k // 2) * 4 + xx * 2 + k % 2, :, rows_of(yy), :],
+            near.at[n, k], send_near.at[n, k], recv_near.at[n, k], target(z, xx, core, yy), MESH,
+        )
+
+    for k in range(count):
+        for n in (2, 0, 1):
+            near_copy(k, n).start()
+    for k in range(count):
+        for n in range(3):
+            near_copy(k, n).wait_recv()
+        own = part[(k // 2) * 4 + x * 2 + k % 2, :, rows_of(y), :].astype(f32)
+        total = (own + near[0, k].astype(f32)) + (near[1, k].astype(f32) + near[2, k].astype(f32))
+        sums[k] = total.astype(sums.dtype)
+        owner = per_side * core + k // 2
+        to_self = jnp.logical_and(z == owner, core == k % 2)
+
+        @pl.when(jnp.logical_not(to_self))
+        def _():
+            pltpu.make_async_remote_copy(
+                sums.at[k], far.at[z], send_far.at[k], recv_far.at[z],
+                target(owner, x, k % 2, y), MESH,
+            ).start()
+
+        @pl.when(to_self)
+        def _():
+            pltpu.make_async_copy(sums.at[k], far.at[z], recv_far.at[z]).start()
+
+    for zz in range(depth):
+        pltpu.make_async_copy(far.at[zz], far.at[zz], recv_far.at[zz]).wait()
+    across = target(z, x, core, 1 - y)
+    levels = part.shape[3]
+
+    def levels_of(yy):
+        return pl.ds(pl.multiple_of(yy * (levels // 2), levels // 2), levels // 2)
+
+    swaps = []
+    for pair in range(columns // 2):
+        pieces = []
+        for k in range(2):
+            value = far[0, 2 * pair + k].astype(f32)
+            for zz in range(1, depth):
+                value = value + far[zz, 2 * pair + k].astype(f32)
+            pieces.append(value)
+        turned[pair] = jnp.concatenate(pieces, axis=0).T
+        swap_out[pair] = turned[pair, levels_of(1 - y), :].astype(swap_out.dtype)
+        copy = pltpu.make_async_remote_copy(
+            swap_out.at[pair], swap_in.at[pair], send_y.at[pair], recv_y.at[pair], across, MESH
+        )
+        copy.start()
+        swaps.append(copy)
+    for pair in range(columns // 2):
+        swaps[pair].wait_recv()
+        mine = turned[pair, levels_of(y), :]
+        theirs = swap_in[pair].astype(f32)
+        low = jnp.where(y == 0, mine, theirs)
+        high = jnp.where(y == 0, theirs, mine)
+        for k in range(2):
+            at = slice(k * half, (k + 1) * half)
+            result[:, 2 * pair + k, :] = jnp.concatenate([low[:, at], high[:, at]], axis=1) * scale
+    for copy in swaps:
+        copy.wait_send()
+    for k in range(count):
+        for n in range(3):
+            near_copy(k, n).wait_send()
+        owner = per_side * core + k // 2
+
+        @pl.when(jnp.logical_not(jnp.logical_and(z == owner, core == k % 2)))
+        def _():
+            pltpu.make_async_copy(sums.at[k], sums.at[k], send_far.at[k]).wait()
+
+
+def gather(part, depth, scale):
+    columns, rows, levels = part.shape[1:]
+    count = depth
+    dma = pltpu.SemaphoreType.DMA
+    piece = (columns, rows // 2, levels)
+    swap = (columns // 2, levels // 2, rows)
+    vmem = pl.BlockSpec(memory_space=pltpu.VMEM)
+    return pl.pallas_call(
+        functools.partial(gather_kernel, depth, scale),
+        out_shape=jax.ShapeDtypeStruct((levels // 2, columns, rows), jnp.float32),
+        in_specs=[vmem],
+        out_specs=vmem,
+        scratch_shapes=[
+            pltpu.VMEM((3, count) + piece, part.dtype),
+            pltpu.VMEM((count,) + piece, part.dtype),
+            pltpu.VMEM((depth,) + piece, part.dtype),
+            pltpu.VMEM((columns // 2, levels, rows), jnp.float32),
+            pltpu.VMEM(swap, part.dtype),
+            pltpu.VMEM(swap, part.dtype),
+            dma((3, count)), dma((3, count)), dma((count,)), dma((depth,)),
+            dma((columns // 2,)), dma((columns // 2,)),
+        ],
+        compiler_params=pltpu.CompilerParams(collective_id=1, has_side_effects=True),
+        cost_estimate=pl.CostEstimate(flops=10**9, bytes_accessed=10**7, transcendentals=0),
+    )(part)
+
+
+def member_increment(
     ens_coarse, col_interp, row_weights, ctrl_vec, band_loc, row_loc, level_loc, total_members
 ):
+    bf16 = jnp.bfloat16
+    tiles = lax.axis_size("tile")
+    depth, chips = tiles // 4, tiles // 2
+    core = lax.rem(lax.axis_index("tile"), 2)
+    columns = band_loc.shape[0]
     fine_rows = row_weights.shape[1]
-    stencil = row_matrix(row_weights, fine_rows, fine_rows // 2).T
-    band = jnp.kron(band_loc, jnp.eye(GROUP, dtype=jnp.bfloat16))
-    ctrl_own = jnp.swapaxes(ctrl_vec[0], 0, 1)
-    ctrl_before, ctrl_after = neighbours(ctrl_own)
-    ctrl = jnp.concatenate([ctrl_before, ctrl_own, ctrl_after], axis=0)
-    members = ens_coarse.shape[1]
-    chunks = CHUNKS if members % CHUNKS == 0 else 1
-    size = members // chunks
+    levels = level_loc.shape[0]
+    members, block_rows = ens_coarse.shape[1], ens_coarse.shape[3]
+    width = ens_coarse.shape[4]
+    own = jnp.transpose(ctrl_vec[0], (1, 2, 0)).astype(bf16).reshape(2, columns // 2 * fine_rows, levels)
+    band = jnp.pad(band_loc, ((0, 16 - columns), (0, levels - band_loc.shape[1])))
+    own = jnp.concatenate([own, jnp.broadcast_to(band, (2,) + band.shape)], axis=1)
+    slots, halo = spread(own, depth)
+    stencil = row_matrix(row_weights, fine_rows, fine_rows // 2)
+    kept = columns * tiles // 2
+    padded = jnp.pad(col_interp, ((columns, columns), (0, 0)))
+    interp = lax.dynamic_slice_in_dim(padded, core * kept, kept + 2 * columns, 0)
+    mixing = jnp.kron(jnp.eye(2, dtype=bf16), level_loc.T)
+    raw = jnp.transpose(ens_coarse[0], (0, 2, 3, 1))
+    per_chip = members // chips
+    raw = raw.reshape(chips, per_chip, 2, block_rows // 2, width, levels)
+    pairs = [(i, i + 1 - 2 * (i % 2)) for i in range(tiles)]
     total = None
-    for chunk in range(chunks):
-        piece = ens_coarse[0, chunk * size : (chunk + 1) * size]
-        coarse_cols = jnp.einsum(
-            "klic,jc->jkil", piece, col_interp, preferred_element_type=jnp.float32
-        ).astype(jnp.bfloat16)
-        peers = lax.axis_size("tile")
-        columns = coarse_cols.shape[0] // peers
-        blocks = coarse_cols.reshape((peers, columns) + coarse_cols.shape[1:])
-        moved = lax.all_to_all(blocks, "tile", split_axis=0, concat_axis=0, tiled=True)
-        own = jnp.transpose(moved, (2, 1, 0, 3, 4))
-        own = own.reshape(size, columns, -1, own.shape[-1])
-        before, after = neighbours(own)
-        part = member_sum(before, own, after, ctrl, stencil, band, row_loc, level_loc)
-        total = part if total is None else total + part
-    return swap_add(jnp.swapaxes(total, 0, 1)) / (total_members - 1)
+    bounds = [0, (per_chip + 1) // 2, per_chip]
+    for low, high in zip(bounds[:-1], bounds[1:]):
+        piece = jnp.swapaxes(raw[:, low:high], 1, 2)
+        piece = piece.reshape((tiles, high - low) + raw.shape[3:])
+        mine = lax.all_to_all(piece, "tile", split_axis=0, concat_axis=0, tiled=True)
+        other = lax.ppermute(mine, "tile", pairs)
+        total = ensemble_sum(mine, other, slots, halo, interp, stencil, row_loc, mixing, total)
+    part = total.reshape(chips, columns, fine_rows, levels)
+    return gather(part, depth, 1.0 / (total_members - 1))
+
+
+def fits(mesh_sizes, members, columns, block_rows, fine_rows, levels):
+    tiles = mesh_sizes["tile"]
+    return (
+        mesh_sizes["grp"] == 1
+        and mesh_sizes["mem"] == 2
+        and tiles % 8 == 0
+        and members % (tiles // 2) == 0
+        and columns == 8
+        and block_rows == 4
+        and fine_rows == 128
+        and levels == 128
+    )
 
 
 def body(
@@ -252,7 +552,12 @@
     )
     sums = jnp.concatenate([gram_sums, right_side[:, :, None]], axis=2)
     sums = swap_add(lax.psum(sums, "grp") if lax.axis_size("grp") > 1 else sums)
-    plan = fused_increment if lax.axis_size("grp") == 1 else plain_increment
+    sizes = {axis: lax.axis_size(axis) for axis in ("grp", "tile", "mem")}
+    plan = plain_increment
+    if fits(
+        sizes, ens_coarse.shape[1], band_loc.shape[0], ens_coarse.shape[3], row_loc.shape[0], level_loc.shape[0]
+    ):
+        plan = member_increment
     increment = plan(
         ens_coarse, col_interp, row_weights, ctrl_vec, band_loc, row_loc, level_loc, total_members
     )

time: 296 us -> 256 us (0.86)
  waiting for transfers between devices: 126 us -> 30 us
  Pallas kernels: 46.5 us -> 135 us
  starting transfers between devices: 32.6 us -> 14.5 us
  local copies, waits for them, and re-layouts: 23.9 us -> 12.3 us
  matrix products: 6.53 us -> 2.17 us
    pallas_call x2 -> x4, Pallas kernels: 46.5 us -> 135 us  [the longest x1 52.5 us: spread(): pl.pallas_call(functools.partial(spread_kernel, depth), out_shape=(jax.Sh...]
    all_to_all x2, waiting for transfers between devices: 89.1 us -> 28.1 us  [member_increment(): lax.all_to_all(piece, 'tile', split_axis=0, concat_axis=0, tiled=True)]
    ppermute x6 -> x2, waiting for transfers between devices: 33.6 us -> 0.01 us  [member_increment(): other = lax.ppermute(mine, 'tile', pairs)]
    ppermute x6 -> x2, starting transfers between devices: 16.4 us -> 0.64 us  [member_increment(): other = lax.ppermute(mine, 'tile', pairs)]
    reshape x2 -> x0, local copies, waits for them, and re-layouts: 9.78 us -> none  [fused_increment(): blocks = coarse_cols.reshape((peers, columns) + coarse_cols.shape[1:])]
    transpose x2 -> x1, local copies, waits for them, and re-layouts: 7.95 us -> 0.11 us  [member_increment(): mixing = jnp.kron(jnp.eye(2, dtype=bf16), level_loc.T)]
    dot_general x2 -> x0, matrix products: 4.36 us -> none  [fused_increment(): jnp.einsum('klic,jc->jkil', piece, col_interp, preferred_element_type=jnp...]
    unnamed x30 -> x35, local copies, waits for them, and re-layouts: 4.77 us -> 7.93 us
  transfers between devices with their start and end apart: 11 -> 6, of which waited for: 4 -> 2; matrix products, arithmetic and copies ran while one was open for 26% -> 26% of each run, Pallas kernels for 8% -> 31%
where the time goes in v1:
time: 256 us; the launch traced here: 255 us
  Pallas kernels  135 us (53%)
  other arithmetic  60 us (23%)
  waiting for transfers between devices  30 us (12%)
  starting transfers between devices  14.5 us (6%)
  local copies, waits for them, and re-layouts  12.3 us (5%)
    pallas_call x1, Pallas kernels, spread(): pl.pallas_call(functools.partial(spread_kernel, depth), out_shape=(jax.Sh...  52.5 us
    pallas_call x2, Pallas kernels, ensemble_sum(): pl.pallas_call(functools.partial(ensemble_kernel, first), grid=(members,)...  44.9 us
    pallas_call x1, Pallas kernels, gather(): pl.pallas_call(functools.partial(gather_kernel, depth, scale), out_shape=...  37.4 us
    another operation x4, other arithmetic, solve_weights(): factor = jnp.linalg.cholesky(system)  30.2 us
    all_to_all x2, waiting for transfers between devices, member_increment(): lax.all_to_all(piece, 'tile', split_axis=0, concat_axis=0, tiled=True)  28.1 us
    another operation x3, other arithmetic, solve_weights(): lax.linalg.triangular_solve(factor, halfway, left_side=True, lower=True,...  26.1 us
    all_to_all x2, starting transfers between devices, member_increment(): lax.all_to_all(piece, 'tile', split_axis=0, concat_axis=0, tiled=True)  12.1 us
    unnamed x35, local copies, waits for them, and re-layouts  7.93 us
  transfers between devices with their start and end apart: 6, of which 2 were waited for; matrix products, arithmetic and copies ran while one was open for 26% of the time, Pallas kernels for 31%

profile of v1, /device:TPU:9, one launch (start us, length us, event | category | flops | bytes accessed | tf_op | source)
XLA Modules:
  0.0 254.9 jit_solution(9022581327589390507)
XLA Ops:
  0.6 1.6 slice.41
  2.3 1.4 copy.35
  3.7 6.7 %all-to-all-start.1 = ((bf16[16,3,2,64,128]{4,3,2,1,0:T(8,128)(2,1)}), bf16[16,3,2,64,128]{4,3,2,1,0:T(8,128)(2,1)S(1)}, u32[]{:S(2)}, u32[]{:S(2)}) async-start(bf16[16,3,2,64,128]{4,3,2,1,0:T(8,128)(2,1)} %bitcast.15), calls=%async_computation.1 | async-start | bytes 3145728 | tf_op jit(solution)/shard_map/all_to_all | solution.py:508
  10.4 0.0 copy-done.6
  10.4 0.0 copy-done.9
  10.4 0.0 copy-done.10
  10.4 0.0 copy-done.14
  10.4 0.3 fusion.6
  10.8 0.1 fusion.5
  10.8 1.2 fusion
  12.1 0.0 copy-start.5
  12.1 0.0 copy-start.7
  12.1 0.7 copy-done.4
  12.8 1.2 collective-permute-start.2
  14.0 1.3 slice.40
  15.3 0.0 copy-done.5
  15.3 0.0 copy-start.12
  15.4 0.2 copy.22
  15.6 0.0 copy-done.7
  15.6 0.1 copy.24
  15.7 1.1 copy.34
  16.8 0.0 copy-done.12
  16.9 0.7 pad_maximum_fusion.own
  17.6 0.2 broadcast_multiply_fusion
  17.8 28.1 %all-to-all-done.1.own = bf16[16,3,2,64,128]{4,3,2,1,0:T(8,128)(2,1)S(1)} async-done(((bf16[16,3,2,64,128]{4,3,2,1,0:T(8,128)(2,1)}), bf16[16,3,2,64,128]{4,3,2,1,0:T(8,128)(2,1)S(1)}, u32[]{:S(2)}, u32[]{:S(2)}) %all-to-all-start.1) | async-done | bytes 1572896 | tf_op jit(solution)/shard_map/all_to_all | solution.py:508
  45.9 5.4 %all-to-all-start = ((bf16[16,2,2,64,128]{4,3,2,1,0:T(8,128)(2,1)}), bf16[16,2,2,64,128]{4,3,2,1,0:T(8,128)(2,1)S(1)}, u32[]{:S(2)}, u32[]{:S(2)}) async-start(bf16[16,2,2,64,128]{4,3,2,1,0:T(8,128)(2,1)} %bitcast.71), calls=%async_computation | async-start | bytes 2097152 | tf_op jit(solution)/shard_map/all_to_all | solution.py:508
  51.3 0.0 copy-start.13
  51.3 52.5 %shard_map.122 = (bf16[8,2,528,128]{3,2,1,0:T(8,128)(2,1)}, bf16[2,528,128]{2,1,0:T(8,128)(2,1)}) custom-call(bf16[2,528,128]{2,1,0:T(8,128)(2,1)} %pad_maximum_fusion.own), custom_call_target="tpu_custom_call" | custom-call | flops 1000000000 | bytes 10000000 | tf_op jit(solution)/shard_map/pallas_call | solution.py:198
  103.8 0.0 copy-start
  103.9 0.0 copy-start.3
  103.9 0.1 copy.27
  104.0 0.0 copy-done.8
  104.0 0.1 copy.23
  104.1 0.0 copy-done.13
  104.2 0.2 add_convert_fusion.stencil
  104.4 0.0 collective-permute-done.2
  104.4 1.0 fusion.12
  105.4 0.4 collective-permute-start.1
  105.9 0.7 slice_add_fusion
  106.6 1.0 copy.28
  107.6 0.7 fusion.16
  108.3 30.1 %custom-call.9 = f32[4,80,80]{2,1,0:T(8,128)S(1)} custom-call(f32[4,80,80]{2,1,0:T(8,128)} %fusion.16), custom_call_target="Cholesky" | custom-call | tf_op jit(solution)/shard_map/jit(cholesky)/cholesky | solution.py:69
  138.4 0.1 compare_reduce_fusion
  138.5 0.8 select_bitcast_fusion
  139.3 25.4 %custom-call.10 = f32[4,1,80,80]{2,3,1,0:T(8,128)S(1)} custom-call(f32[4,1,80,80]{3,2,1,0:T(8,128)} %select_bitcast_fusion), custom_call_target="InvertDiagBlocksLowerTriangular" | custom-call | tf_op jit(solution)/shard_map/triangular_solve | solution.py:71
  164.6 0.0 all-to-all-done.own
  164.6 0.2 collective-permute-start
  164.8 0.3 convolution_bitcast_fusion
  165.1 0.4 fusion.13
  165.5 0.5 collective-permute-start.3
  166.0 1.9 collective-permute-done.3
  167.9 0.0 collective-permute-done.1.other
  167.9 0.0 copy-done
  168.0 0.0 copy-done.3
  168.0 0.0 copy-start.2
  168.0 1.6 copy-done.2
  169.6 26.9 %shard_map.123.start = bf16[64,128,128]{2,1,0:T(8,128)(2,1)S(1)} custom-call(bf16[16,3,2,64,128]{4,3,2,1,0:T(8,128)(2,1)S(1)} %all-to-all-done.1.own, bf16[16,3,2,64,128]{4,3,2,1,0:T(8,128)(2,1)} %collective-permute-done.1.other, bf16[8,2,528,128]{3,2,1,0:T(8,128)(2,1)S(1)} %copy-done.2, bf16[2,528,128]{2,1,0:T(8,128)(2,1)S(1)} %copy-done.3, ...), custom_call_target="tpu_custom_call" | custom-call | flops 5536481280 | bytes 3145728 | tf_op jit(solution)/shard_map/pallas_call | solution.py:335
  196.5 0.0 copy-done.11
  196.5 0.0 collective-permute-done.other
  196.5 18.0 %shard_map.124 = bf16[64,128,128]{2,1,0:T(8,128)(2,1)S(1)} custom-call(bf16[16,2,2,64,128]{4,3,2,1,0:T(8,128)(2,1)S(1)} %all-to-all-done.own, bf16[16,2,2,64,128]{4,3,2,1,0:T(8,128)(2,1)S(1)} %collective-permute-done.other, bf16[8,2,528,128]{3,2,1,0:T(8,128)(2,1)S(1)} %copy-done.2, bf16[2,528,128]{2,1,0:T(8,128)(2,1)S(1)} %copy-done.3, ...), custom_call_target="tpu_custom_call" | custom-call | flops 3690987520 | bytes 2097152 | tf_op jit(solution)/shard_map/pallas_call | solution.py:335
  214.5 0.0 copy-start.1
  214.5 1.3 copy-done.1
  215.8 37.4 %shard_map.125 = f32[64,8,128]{2,1,0:T(8,128)} custom-call(bf16[8,8,128,128]{3,2,1,0:T(8,128)(2,1)} %bitcast.70), custom_call_target="tpu_custom_call" | custom-call | flops 1000000000 | bytes 10000000 | tf_op jit(solution)/shard_map/pallas_call | solution.py:458
  253.2 1.7 copy.42
  (27 shorter events, 0.3 us)
Async XLA Ops:
  3.6 6.7 %copy-start.6 = (bf16[1,80,2048]{2,1,0:T(8,128)(2,1)S(1)}, bf16[1,80,2048]{2,1,0:T(8,128)(2,1)}, u32[]{:S(2)}) copy-start(bf16[1,80,2048]{2,1,0:T(8,128)(2,1)} %param.18) | copy-start | bytes 983044
  3.6 6.7 %copy-start.9 = (s32[1,2048]{1,0:T(1,128)S(1)}, s32[1,2048]{1,0:T(1,128)}, u32[]{:S(2)}) copy-start(s32[1,2048]{1,0:T(1,128)} %param.21) | copy-start | bytes 24580
  3.7 6.7 %copy-start.10 = (f32[1,2048]{1,0:T(1,128)S(1)}, f32[1,2048]{1,0:T(1,128)}, u32[]{:S(2)}) copy-start(f32[1,2048]{1,0:T(1,128)} %param.20) | copy-start | bytes 24580
  3.7 6.7 %copy-start.14 = (f32[1,2048]{1,0:T(1,128)S(1)}, f32[1,2048]{1,0:T(1,128)}, u32[]{:S(2)}) copy-start(f32[1,2048]{1,0:T(1,128)} %param.19) | copy-start | bytes 24580
  3.7 42.2 %all-to-all-start.1 = ((bf16[16,3,2,64,128]{4,3,2,1,0:T(8,128)(2,1)}), bf16[16,3,2,64,128]{4,3,2,1,0:T(8,128)(2,1)S(1)}, u32[]{:S(2)}, u32[]{:S(2)}) async-start(bf16[16,3,2,64,128]{4,3,2,1,0:T(8,128)(2,1)} %bitcast.15), calls=%async_computation.1 | async-start | bytes 3145728 | tf_op jit(solution)/shard_map/all_to_all | solution.py:508
  12.0 0.7 copy-start.4
  12.1 3.3 %copy-start.5 = (f32[1,128,8,128]{3,2,1,0:T(8,128)S(1)}, f32[1,128,8,128]{3,2,1,0:T(8,128)}, u32[]{:S(2)}) copy-start(f32[1,128,8,128]{3,2,1,0:T(8,128)} %param.14) | copy-start | bytes 1572868
  12.1 3.6 %copy-start.7 = (bf16[128,128]{1,0:T(8,128)(2,1)S(1)}, bf16[128,128]{1,0:T(8,128)(2,1)}, u32[]{:S(2)}) copy-start(bf16[128,128]{1,0:T(8,128)(2,1)} %param.17) | copy-start | bytes 98308
  12.8 91.6 %collective-permute-start.2 = (f32[4,80,81]{1,2,0:T(8,128)S(1)}, f32[4,80,81]{1,2,0:T(8,128)}, u32[]{:S(2)}, u32[]{:S(2)}) collective-permute-start(f32[4,80,81]{1,2,0:T(8,128)S(1)} %fusion.10), channel_id=1, source_target_pairs={{0,1},{1,0},{2,3},{3,2},{4,5},{5,4},{6,7},{7,6},{8,9},{9,8},{10,11... | collective-permute-start | bytes 311048 | tf_op jit(solution)/shard_map/ppermute | solution.py:37
  15.3 1.5 copy-start.12
  45.9 118.7 %all-to-all-start = ((bf16[16,2,2,64,128]{4,3,2,1,0:T(8,128)(2,1)}), bf16[16,2,2,64,128]{4,3,2,1,0:T(8,128)(2,1)S(1)}, u32[]{:S(2)}, u32[]{:S(2)}) async-start(bf16[16,2,2,64,128]{4,3,2,1,0:T(8,128)(2,1)} %bitcast.71), calls=%async_computation | async-start | bytes 2097152 | tf_op jit(solution)/shard_map/all_to_all | solution.py:508
  51.3 52.6 %copy-start.8 = (bf16[128,64]{0,1:T(8,128)(2,1)S(1)}, bf16[128,64]{0,1:T(8,128)(2,1)}, u32[]{:S(2)}) copy-start(bf16[128,64]{0,1:T(8,128)(2,1)} %param.12) | copy-start | bytes 49156
  51.3 52.8 %copy-start.13 = (bf16[3,128]{1,0:T(4,128)(2,1)S(1)}, bf16[3,128]{1,0:T(4,128)(2,1)}, u32[]{:S(2)}) copy-start(bf16[3,128]{1,0:T(4,128)(2,1)} %param.13) | copy-start | bytes 2308
  103.8 64.1 %copy-start = (bf16[128,128]{1,0:T(8,128)(2,1)S(1)}, bf16[128,128]{1,0:T(8,128)(2,1)}, u32[]{:S(2)}) copy-start(bf16[128,128]{1,0:T(8,128)(2,1)} %row_loc.3) | copy-start | bytes 98308
  103.9 64.1 %copy-start.3 = (bf16[2,528,128]{2,1,0:T(8,128)(2,1)S(1)}, bf16[2,528,128]{2,1,0:T(8,128)(2,1)}, u32[]{:S(2)}) copy-start(bf16[2,528,128]{2,1,0:T(8,128)(2,1)} %get-tuple-element.5.halo) | copy-start | bytes 811012
  105.4 62.5 %collective-permute-start.1 = (bf16[16,3,2,64,128]{4,3,2,1,0:T(8,128)(2,1)S(1)}, bf16[16,3,2,64,128]{4,3,2,1,0:T(8,128)(2,1)}, u32[]{:S(2)}, u32[]{:S(2)}) collective-permute-start(bf16[16,3,2,64,128]{4,3,2,1,0:T(8,128)(2,1)S(1)} %all-to-all-done.1.own), channel_id=1, source_target_pairs={{0,2},{2,0},{4,6},{6,4},{8,10},{10,8},{12,14},{14,12},{16,18},{18,... | collective-permute-start | bytes 4718600 | tf_op jit(solution)/shard_map/ppermute | solution.py:509
  164.6 31.9 %collective-permute-start = (bf16[16,2,2,64,128]{4,3,2,1,0:T(8,128)(2,1)S(1)}, bf16[16,2,2,64,128]{4,3,2,1,0:T(8,128)(2,1)S(1)}, u32[]{:S(2)}, u32[]{:S(2)}) collective-permute-start(bf16[16,2,2,64,128]{4,3,2,1,0:T(8,128)(2,1)S(1)} %all-to-all-done.own), channel_id=1, source_target_pairs={{0,2},{2,0},{4,6},{6,4},{8,10},{10,8},{12,14},{14,12},{16,18},{18,... | collective-permute-start | bytes 3145736 | tf_op jit(solution)/shard_map/ppermute | solution.py:509
  165.5 2.5 collective-permute-start.3
  167.9 28.6 %copy-start.11 = (f32[8,80]{1,0:T(8,128)}, f32[8,80]{1,0:T(8,128)S(1)}, u32[]{:S(2)}) copy-start(f32[8,80]{1,0:T(8,128)S(1)} %constant_dynamic-update-slice_fusion) | copy-start | bytes 7684
  168.0 1.6 copy-start.2
  214.5 1.3 copy-start.1

commit v2 on v1

--- a/solution.py
+++ b/solution.py
@@ -63,15 +63,43 @@
     return stencil.astype(jnp.bfloat16)
 
 
-def solve_weights(gram_sums, right_side):
-    member_count = gram_sums.shape[-1]
-    system = gram_sums + (member_count - 1) * jnp.eye(member_count, dtype=jnp.float32)
-    factor = jnp.linalg.cholesky(system)
-    halfway = lax.linalg.triangular_solve(factor, right_side[..., None], left_side=True, lower=True)
-    result = lax.linalg.triangular_solve(
-        factor, halfway, left_side=True, lower=True, transpose_a=True
-    )
-    return result[..., 0]
+def solve_kernel(sums, result):
+    regions, members, lanes = sums.shape
+    row_index = lax.broadcasted_iota(jnp.int32, (members, lanes), 0)
+    col_index = lax.broadcasted_iota(jnp.int32, (members, lanes), 1)
+    tables = []
+    for region in range(regions):
+        table = sums[region]
+        square = jnp.concatenate([table, jnp.zeros((lanes - members, lanes), jnp.float32)], axis=0)
+        mirrored = square.T[:members]
+        table = jnp.where(col_index < members, 0.5 * (table + mirrored), table)
+        tables.append(table + jnp.where(row_index == col_index, float(members - 1), 0.0))
+    for k in range(members):
+        for region in range(regions):
+            table = tables[region]
+            row = table[k : k + 1]
+            pivot = row[:, k : k + 1]
+            row = row / pivot
+            column = table[:, k : k + 1] - jnp.where(row_index[:, :1] == k, 1.0, 0.0)
+            tables[region] = table - column * row
+    for region in range(regions):
+        result[region] = jnp.concatenate(
+            [tables[region], jnp.zeros((lanes - members, lanes), jnp.float32)], axis=0
+        ).T[members : members + 8, :]
+
+
+def solve_weights(sums):
+    regions, members, width = sums.shape
+    lanes = 128 * (-(-(members + 8) // 128))
+    padded = jnp.pad(sums, ((0, 0), (0, 0), (0, lanes - width)))
+    result = pl.pallas_call(
+        solve_kernel,
+        out_shape=jax.ShapeDtypeStruct((regions, 8, lanes), jnp.float32),
+        in_specs=[pl.BlockSpec(memory_space=pltpu.VMEM)],
+        out_specs=pl.BlockSpec(memory_space=pltpu.VMEM),
+        cost_estimate=pl.CostEstimate(flops=10**9, bytes_accessed=4 * padded.size, transcendentals=0),
+    )(padded)
+    return result[:, 0, :members]
 
 
 def plain_increment(
@@ -561,7 +589,7 @@
     increment = plan(
         ens_coarse, col_interp, row_weights, ctrl_vec, band_loc, row_loc, level_loc, total_members
     )
-    own_weights = solve_weights(sums[:, :, :total_members], sums[:, :, total_members])
+    own_weights = solve_weights(sums)
     weights = collect(own_weights)
     return (increment[None], weights)
 

time: 256 us -> 208 us (0.81)
  other arithmetic: 60 us -> 7.85 us
  waiting for transfers between devices: 30 us -> 34.4 us
  local copies, waits for them, and re-layouts: 12.3 us -> 15.7 us
  Pallas kernels: 135 us -> 132 us
    another operation x7 -> x0, other arithmetic: 56.4 us -> none  [the longest x4 30.2 us: solve_weights(): factor = jnp.linalg.cholesky(system)]
    pallas_call x1, Pallas kernels: 52.5 us -> 38.5 us  [spread(): pl.pallas_call(functools.partial(spread_kernel, depth), out_shape=(jax.Sh...]
    pallas_call x0 -> x1, Pallas kernels: none -> 10.2 us  [solve_weights(): pl.pallas_call(solve_kernel, out_shape=jax.ShapeDtypeStruct((regions, 8,...]
    all_to_all x2, waiting for transfers between devices: 28.1 us -> 32.2 us  [member_increment(): lax.all_to_all(piece, 'tile', split_axis=0, concat_axis=0, tiled=True)]
    unnamed x35 -> x29, local copies, waits for them, and re-layouts: 7.93 us -> 8.75 us
  transfers between devices with their start and end apart: 6 -> 6, of which waited for: 2 -> 2; matrix products, arithmetic and copies ran while one was open for 26% -> 9% of each run, Pallas kernels for 31% -> 36%
where the time goes in v2:
time: 208 us; the launch traced here: 207 us
  Pallas kernels  132 us (63%)
  waiting for transfers between devices  34.4 us (17%)
  local copies, waits for them, and re-layouts  15.7 us (8%)
  starting transfers between devices  14.6 us (7%)
  other arithmetic  7.85 us (4%)
  matrix products  2.26 us (1%)
    pallas_call x2, Pallas kernels, ensemble_sum(): pl.pallas_call(functools.partial(ensemble_kernel, first), grid=(members,)...  45.6 us
    pallas_call x1, Pallas kernels, spread(): pl.pallas_call(functools.partial(spread_kernel, depth), out_shape=(jax.Sh...  38.5 us
    pallas_call x1, Pallas kernels, gather(): pl.pallas_call(functools.partial(gather_kernel, depth, scale), out_shape=...  37.2 us
    all_to_all x2, waiting for transfers between devices, member_increment(): lax.all_to_all(piece, 'tile', split_axis=0, concat_axis=0, tiled=True)  32.2 us
    all_to_all x2, starting transfers between devices, member_increment(): lax.all_to_all(piece, 'tile', split_axis=0, concat_axis=0, tiled=True)  12 us
    pallas_call x1, Pallas kernels, solve_weights(): pl.pallas_call(solve_kernel, out_shape=jax.ShapeDtypeStruct((regions, 8,...  10.2 us
    unnamed x29, local copies, waits for them, and re-layouts  8.75 us
  transfers between devices with their start and end apart: 6, of which 2 were waited for; matrix products, arithmetic and copies ran while one was open for 9% of the time, Pallas kernels for 36%

profile of v2, /device:TPU:9, one launch (start us, length us, event | category | flops | bytes accessed | tf_op | source)
XLA Modules:
  0.0 207.3 jit_solution(17144261669548054220)
XLA Ops:
  0.6 1.6 slice.25
  2.3 1.4 copy.25
  3.6 6.5 %all-to-all-start.1 = ((bf16[16,3,2,64,128]{4,3,2,1,0:T(8,128)(2,1)}), bf16[16,3,2,64,128]{4,3,2,1,0:T(8,128)(2,1)S(1)}, u32[]{:S(2)}, u32[]{:S(2)}) async-start(bf16[16,3,2,64,128]{4,3,2,1,0:T(8,128)(2,1)} %bitcast.15), calls=%async_computation.1 | async-start | bytes 3145728 | tf_op jit(solution)/shard_map/all_to_all | solution.py:536
  10.2 0.0 copy-start.8
  10.2 0.0 copy-start.4
  10.2 0.0 copy-start.9
  10.2 1.4 slice.24
  11.6 0.0 copy-start.11
  11.6 1.1 copy.24
  12.7 0.0 copy-done.8
  12.7 0.0 copy-done.4
  12.7 0.0 copy-done.9
  12.7 0.8 fusion.5
  13.5 32.2 %all-to-all-done.1.own = bf16[16,3,2,64,128]{4,3,2,1,0:T(8,128)(2,1)S(1)} async-done(((bf16[16,3,2,64,128]{4,3,2,1,0:T(8,128)(2,1)}), bf16[16,3,2,64,128]{4,3,2,1,0:T(8,128)(2,1)S(1)}, u32[]{:S(2)}, u32[]{:S(2)}) %all-to-all-start.1) | async-done | bytes 1572896 | tf_op jit(solution)/shard_map/all_to_all | solution.py:536
  45.7 5.4 %all-to-all-start = ((bf16[16,2,2,64,128]{4,3,2,1,0:T(8,128)(2,1)}), bf16[16,2,2,64,128]{4,3,2,1,0:T(8,128)(2,1)S(1)}, u32[]{:S(2)}, u32[]{:S(2)}) async-start(bf16[16,2,2,64,128]{4,3,2,1,0:T(8,128)(2,1)} %bitcast.49), calls=%async_computation | async-start | bytes 2097152 | tf_op jit(solution)/shard_map/all_to_all | solution.py:536
  51.1 0.0 copy-done.11
  51.2 0.4 convolution_bitcast_fusion
  51.5 0.2 copy.23
  51.7 0.0 copy-start.6
  51.7 0.0 copy-start.7
  51.7 1.9 fusion
  53.7 0.8 fusion.9
  54.5 1.2 collective-permute-start.2
  55.7 0.0 copy-done.6
  55.7 0.7 copy.21
  56.4 1.1 convert_bitcast_fusion
  57.5 0.7 collective-permute-start.1
  58.2 1.6 broadcast_multiply_fusion
  59.8 0.0 copy-done.7
  59.8 0.7 copy.20
  60.5 0.7 convert_element_type.44
  61.2 0.9 copy.19
  62.1 0.9 copy.28
  63.0 0.7 pad.12
  63.7 0.0 copy-start.5
  63.7 1.7 pad_maximum_fusion.own
  65.4 38.5 %shard_map.122 = (bf16[8,2,528,128]{3,2,1,0:T(8,128)(2,1)}, bf16[2,528,128]{2,1,0:T(8,128)(2,1)}) custom-call(bf16[2,528,128]{2,1,0:T(8,128)(2,1)} %pad_maximum_fusion.own), custom_call_target="tpu_custom_call" | custom-call | flops 1000000000 | bytes 10000000 | tf_op jit(solution)/shard_map/pallas_call | solution.py:226
  104.0 0.2 add_convert_fusion.stencil
  104.2 0.0 copy-done.5
  104.2 0.0 all-to-all-done.own
  104.2 0.4 collective-permute-start
  104.7 0.0 collective-permute-done.2
  104.7 1.0 fusion.11
  105.7 0.0 copy-start
  105.7 0.0 copy-start.3
  105.7 0.7 pad.14.sums
  106.4 10.2 %shard_map.126 = f32[4,8,128]{2,1,0:T(8,128)} custom-call(f32[4,80,128]{2,1,0:T(8,128)} %pad.14.sums), custom_call_target="tpu_custom_call" | custom-call | flops 1000000000 | bytes 163840 | tf_op jit(solution)/shard_map/pallas_call | solution.py:95
  116.6 0.7 slice.26
  117.3 0.2 collective-permute-start.3
  117.5 2.2 %collective-permute-done.3 = f32[4,80]{1,0:T(4,128)S(1)} collective-permute-done((f32[4,80]{1,0:T(4,128)S(1)}, f32[4,80]{1,0:T(4,128)S(1)}, u32[]{:S(2)}, u32[]{:S(2)}) %collective-permute-start.3) | collective-permute-done | bytes 1312 | tf_op jit(solution)/shard_map/ppermute | solution.py:49
  119.7 0.0 copy-start.10
  119.7 0.0 collective-permute-done.1.other
  119.8 0.0 copy-done
  119.8 0.0 copy-done.3
  119.8 0.0 copy-start.2
  119.8 1.6 copy-done.2
  121.4 26.8 %shard_map.123.start = bf16[64,128,128]{2,1,0:T(8,128)(2,1)S(1)} custom-call(bf16[16,3,2,64,128]{4,3,2,1,0:T(8,128)(2,1)S(1)} %all-to-all-done.1.own, bf16[16,3,2,64,128]{4,3,2,1,0:T(8,128)(2,1)} %collective-permute-done.1.other, bf16[8,2,528,128]{3,2,1,0:T(8,128)(2,1)S(1)} %copy-done.2, bf16[2,528,128]{2,1,0:T(8,128)(2,1)S(1)} %copy-done.3, ...), custom_call_target="tpu_custom_call" | custom-call | flops 5536481280 | bytes 3145728 | tf_op jit(solution)/shard_map/pallas_call | solution.py:363
  148.2 0.0 copy-done.10
  148.2 0.0 collective-permute-done.other
  148.2 18.8 %shard_map.124 = bf16[64,128,128]{2,1,0:T(8,128)(2,1)S(1)} custom-call(bf16[16,2,2,64,128]{4,3,2,1,0:T(8,128)(2,1)S(1)} %all-to-all-done.own, bf16[16,2,2,64,128]{4,3,2,1,0:T(8,128)(2,1)} %collective-permute-done.other, bf16[8,2,528,128]{3,2,1,0:T(8,128)(2,1)S(1)} %copy-done.2, bf16[2,528,128]{2,1,0:T(8,128)(2,1)S(1)} %copy-done.3, ...), custom_call_target="tpu_custom_call" | custom-call | flops 3690987520 | bytes 2097152 | tf_op jit(solution)/shard_map/pallas_call | solution.py:363
  167.1 0.0 copy-start.1
  167.1 1.3 copy-done.1
  168.4 37.2 %shard_map.125 = f32[64,8,128]{2,1,0:T(8,128)} custom-call(bf16[8,8,128,128]{3,2,1,0:T(8,128)(2,1)} %bitcast.48), custom_call_target="tpu_custom_call" | custom-call | flops 1000000000 | bytes 10000000 | tf_op jit(solution)/shard_map/pallas_call | solution.py:486
  205.6 1.7 copy.32
  (11 shorter events, 0.1 us)
Async XLA Ops:
  3.6 42.1 %all-to-all-start.1 = ((bf16[16,3,2,64,128]{4,3,2,1,0:T(8,128)(2,1)}), bf16[16,3,2,64,128]{4,3,2,1,0:T(8,128)(2,1)S(1)}, u32[]{:S(2)}, u32[]{:S(2)}) async-start(bf16[16,3,2,64,128]{4,3,2,1,0:T(8,128)(2,1)} %bitcast.15), calls=%async_computation.1 | async-start | bytes 3145728 | tf_op jit(solution)/shard_map/all_to_all | solution.py:536
  10.2 2.5 %copy-start.8 = (s32[1,2048]{1,0:T(1,128)S(1)}, s32[1,2048]{1,0:T(1,128)}, u32[]{:S(2)}) copy-start(s32[1,2048]{1,0:T(1,128)} %param.21) | copy-start | bytes 24580
  10.2 2.5 %copy-start.4 = (bf16[1,80,2048]{2,1,0:T(8,128)(2,1)S(1)}, bf16[1,80,2048]{2,1,0:T(8,128)(2,1)}, u32[]{:S(2)}) copy-start(bf16[1,80,2048]{2,1,0:T(8,128)(2,1)} %param.18) | copy-start | bytes 983044
  10.2 2.5 %copy-start.9 = (f32[1,2048]{1,0:T(1,128)S(1)}, f32[1,2048]{1,0:T(1,128)}, u32[]{:S(2)}) copy-start(f32[1,2048]{1,0:T(1,128)} %param.20) | copy-start | bytes 24580
  11.6 39.6 %copy-start.11 = (f32[1,2048]{1,0:T(1,128)S(1)}, f32[1,2048]{1,0:T(1,128)}, u32[]{:S(2)}) copy-start(f32[1,2048]{1,0:T(1,128)} %param.19) | copy-start | bytes 24580
  45.7 58.5 %all-to-all-start = ((bf16[16,2,2,64,128]{4,3,2,1,0:T(8,128)(2,1)}), bf16[16,2,2,64,128]{4,3,2,1,0:T(8,128)(2,1)S(1)}, u32[]{:S(2)}, u32[]{:S(2)}) async-start(bf16[16,2,2,64,128]{4,3,2,1,0:T(8,128)(2,1)} %bitcast.49), calls=%async_computation | async-start | bytes 2097152 | tf_op jit(solution)/shard_map/all_to_all | solution.py:536
  51.7 4.0 %copy-start.6 = (bf16[128,128]{1,0:T(8,128)(2,1)S(1)}, bf16[128,128]{1,0:T(8,128)(2,1)}, u32[]{:S(2)}) copy-start(bf16[128,128]{1,0:T(8,128)(2,1)} %param.17) | copy-start | bytes 98308
  51.7 8.1 %copy-start.7 = (bf16[128,64]{0,1:T(8,128)(2,1)S(1)}, bf16[128,64]{0,1:T(8,128)(2,1)}, u32[]{:S(2)}) copy-start(bf16[128,64]{0,1:T(8,128)(2,1)} %param.12) | copy-start | bytes 49156
  54.5 50.2 %collective-permute-start.2 = (f32[4,80,81]{2,1,0:T(8,128)}, f32[4,80,81]{2,1,0:T(8,128)}, u32[]{:S(2)}, u32[]{:S(2)}) collective-permute-start(f32[4,80,81]{2,1,0:T(8,128)} %fusion.9), channel_id=1, source_target_pairs={{0,1},{1,0},{2,3},{3,2},{4,5},{5,4},{6,7},{7,6},{8,9},{9,8},{10,11... | collective-permute-start | bytes 311048 | tf_op jit(solution)/shard_map/ppermute | solution.py:37
  57.5 62.2 %collective-permute-start.1 = (bf16[16,3,2,64,128]{4,3,2,1,0:T(8,128)(2,1)S(1)}, bf16[16,3,2,64,128]{4,3,2,1,0:T(8,128)(2,1)}, u32[]{:S(2)}, u32[]{:S(2)}) collective-permute-start(bf16[16,3,2,64,128]{4,3,2,1,0:T(8,128)(2,1)S(1)} %all-to-all-done.1.own), channel_id=1, source_target_pairs={{0,2},{2,0},{4,6},{6,4},{8,10},{10,8},{12,14},{14,12},{16,18},{18,... | collective-permute-start | bytes 4718600 | tf_op jit(solution)/shard_map/ppermute | solution.py:537
  63.7 40.4 %copy-start.5 = (bf16[128,64]{1,0:T(8,128)(2,1)S(1)}, bf16[128,64]{1,0:T(8,128)(2,1)}, u32[]{:S(2)}) copy-start(bf16[128,64]{1,0:T(8,128)(2,1)} %copy.20) | copy-start | bytes 49156
  104.2 44.0 %collective-permute-start = (bf16[16,2,2,64,128]{4,3,2,1,0:T(8,128)(2,1)S(1)}, bf16[16,2,2,64,128]{4,3,2,1,0:T(8,128)(2,1)}, u32[]{:S(2)}, u32[]{:S(2)}) collective-permute-start(bf16[16,2,2,64,128]{4,3,2,1,0:T(8,128)(2,1)S(1)} %all-to-all-done.own), channel_id=1, source_target_pairs={{0,2},{2,0},{4,6},{6,4},{8,10},{10,8},{12,14},{14,12},{16,18},{18,... | collective-permute-start | bytes 3145736 | tf_op jit(solution)/shard_map/ppermute | solution.py:537
  105.7 14.1 %copy-start = (bf16[128,128]{1,0:T(8,128)(2,1)S(1)}, bf16[128,128]{1,0:T(8,128)(2,1)}, u32[]{:S(2)}) copy-start(bf16[128,128]{1,0:T(8,128)(2,1)} %row_loc.3) | copy-start | bytes 98308
  105.7 14.1 %copy-start.3 = (bf16[2,528,128]{2,1,0:T(8,128)(2,1)S(1)}, bf16[2,528,128]{2,1,0:T(8,128)(2,1)}, u32[]{:S(2)}) copy-start(bf16[2,528,128]{2,1,0:T(8,128)(2,1)} %get-tuple-element.5.halo) | copy-start | bytes 811012
  117.3 2.4 %collective-permute-start.3 = (f32[4,80]{1,0:T(4,128)S(1)}, f32[4,80]{1,0:T(4,128)S(1)}, u32[]{:S(2)}, u32[]{:S(2)}) collective-permute-start(f32[4,80]{1,0:T(4,128)S(1)} %bitcast.58), channel_id=1, source_target_pairs={{0,1},{1,0},{2,3},{3,2},{4,5},{5,4},{6,7},{7,6},{8,9},{9,8},{10,11... | collective-permute-start | bytes 3848 | tf_op jit(solution)/shard_map/ppermute | solution.py:49
  119.7 28.5 %copy-start.10 = (f32[8,80]{1,0:T(8,128)}, f32[8,80]{1,0:T(8,128)S(1)}, u32[]{:S(2)}) copy-start(f32[8,80]{1,0:T(8,128)S(1)} %constant_dynamic-update-slice_fusion) | copy-start | bytes 7684
  119.8 1.6 copy-start.2
  167.1 1.3 copy-start.1

commit v3 on v2

v3 whole, which is shorter than its diff:
```python
import functools

import jax
import jax.numpy as jnp
from jax import lax
from jax.experimental import pallas as pl
from jax.experimental.pallas import tpu as pltpu
from jax.sharding import PartitionSpec as P

NREG = 8
GROUP = 16
MESH = pl.DeviceIdType.MESH


def extended(value, sides, width):
    for axis, dim in sides:
        peers, length = (lax.axis_size(axis), value.shape[dim])
        up = [(i, (i + 1) % peers) for i in range(peers - 1)]
        down = [(j, i) for i, j in up]
        last = lax.slice_in_dim(value, length - width, length, axis=dim)
        first = lax.slice_in_dim(value, 0, width, axis=dim)
        before = lax.ppermute(last, axis, up)
        after = lax.ppermute(first, axis, down)
        value = jnp.concatenate([before, value, after], axis=dim)
    return value


def swap_add(value):
    peers = lax.axis_size("mem")
    me = lax.axis_index("mem")
    length = value.shape[0] // peers
    total = lax.dynamic_slice_in_dim(value, me * length, length, 0)
    for shift in range(1, peers):
        other = lax.rem(me + shift, peers)
        part = lax.dynamic_slice_in_dim(value, other * length, length, 0)
        pairs = [(i, (i + shift) % peers) for i in range(peers)]
        total = total + lax.ppermute(part, "mem", pairs)
    return total


def collect(value):
    peers = lax.axis_size("mem")
    me = lax.axis_index("mem")
    length = value.shape[0]
    result = jnp.zeros((peers * length,) + value.shape[1:], value.dtype)
    result = lax.dynamic_update_slice_in_dim(result, value, me * length, 0)
    for shift in range(1, peers):
        pairs = [(i, (i + shift) % peers) for i in range(peers)]
        moved = lax.ppermute(value, "mem", pairs)
        source = lax.rem(me + peers - shift, peers)
        result = lax.dynamic_update_slice_in_dim(result, moved, source * length, 0)
    return result


def row_matrix(row_weights, fine_rows, coarse_rows):
    fine_index = lax.broadcasted_iota(jnp.int32, (fine_rows, coarse_rows), 0)
    coarse_index = lax.broadcasted_iota(jnp.int32, (fine_rows, coarse_rows), 1)
    weights = row_weights.astype(jnp.float32)
    stencil = jnp.zeros((fine_rows, coarse_rows), jnp.float32)
    for offset in range(3):
        matched = coarse_index == fine_index // 2 + offset - 1
        stencil = stencil + jnp.where(matched, weights[offset][:, None], 0.0)
    return stencil.astype(jnp.bfloat16)


def solve_kernel(sums, result):
    regions, members, lanes = sums.shape
    row_index = lax.broadcasted_iota(jnp.int32, (members, lanes), 0)
    col_index = lax.broadcasted_iota(jnp.int32, (members, lanes), 1)
    tables = []
    for region in range(regions):
        table = sums[region]
        square = jnp.concatenate([table, jnp.zeros((lanes - members, lanes), jnp.float32)], axis=0)
        mirrored = square.T[:members]
        table = jnp.where(col_index < members, 0.5 * (table + mirrored), table)
        tables.append(table + jnp.where(row_index == col_index, float(members - 1), 0.0))
    for k in range(members):
        for region in range(regions):
            table = tables[region]
            row = table[k : k + 1]
            pivot = row[:, k : k + 1]
            row = row / pivot
            column = table[:, k : k + 1] - jnp.where(row_index[:, :1] == k, 1.0, 0.0)
            tables[region] = table - column * row
    for region in range(regions):
        result[region] = jnp.concatenate(
            [tables[region], jnp.zeros((lanes - members, lanes), jnp.float32)], axis=0
        ).T[members : members + 8, :]


def solve_weights(sums):
    regions, members, width = sums.shape
    lanes = 128 * (-(-(members + 8) // 128))
    padded = jnp.pad(sums, ((0, 0), (0, 0), (0, lanes - width)))
    result = pl.pallas_call(
        solve_kernel,
        out_shape=jax.ShapeDtypeStruct((regions, 8, lanes), jnp.float32),
        in_specs=[pl.BlockSpec(memory_space=pltpu.VMEM)],
        out_specs=pl.BlockSpec(memory_space=pltpu.VMEM),
        cost_estimate=pl.CostEstimate(flops=10**9, bytes_accessed=4 * padded.size, transcendentals=0),
    )(padded)
    return result[:, 0, :members]


def plain_increment(
    ens_coarse, col_interp, row_weights, ctrl_vec, band_loc, row_loc, level_loc, total_members
):
    fine_rows = row_weights.shape[1]
    columns = band_loc.shape[0]
    coarse_cols = jnp.einsum(
        "tklic,jc->tklij", ens_coarse, col_interp, preferred_element_type=jnp.float32
    ).astype(jnp.bfloat16)
    stencil = row_matrix(row_weights, fine_rows, fine_rows // 2)
    refined = jnp.einsum(
        "tklij,ri->tkljr",
        lax.all_to_all(coarse_cols, "tile", split_axis=4, concat_axis=3, tiled=True),
        stencil,
        preferred_element_type=jnp.float32,
    ).astype(jnp.bfloat16)
    member_fine = refined[0]
    slot_term = member_fine * ctrl_vec[0][None]
    projected = slot_term.astype(jnp.bfloat16)
    if lax.axis_size("grp") > 1:
        projected = lax.psum(projected, "grp")
    padded = extended(projected, (("tile", 2),), columns)
    banded = jnp.einsum(
        "jq,klqr->kljr", band_loc, padded, preferred_element_type=jnp.float32
    ).astype(jnp.bfloat16)
    row_mixed = jnp.einsum(
        "kljs,rs->kljr", banded, row_loc, preferred_element_type=jnp.float32
    ).astype(jnp.bfloat16)
    localized = jnp.einsum(
        "lm,kmjr->kljr", level_loc, row_mixed, preferred_element_type=jnp.float32
    ).astype(jnp.bfloat16)
    return swap_add(
        jnp.sum(member_fine.astype(jnp.float32) * localized.astype(jnp.float32), axis=0)
    ) / (total_members - 1)


def place():
    tile = lax.axis_index("tile")
    core = lax.rem(tile, 2)
    chip = lax.div(tile, 2)
    return lax.div(chip, 2), lax.rem(chip, 2), core, lax.axis_index("mem")


def target(z, x, core, y):
    return {"tile": (z * 2 + x) * 2 + core, "mem": y}


def greet(peers):
    barrier = pltpu.get_barrier_semaphore()
    for peer in peers:
        pl.semaphore_signal(barrier, inc=1, device_id=peer, device_id_type=MESH)
    pl.semaphore_wait(barrier, len(peers))


def fused_kernel(
    depth, scale, raw, own, interp, stencil, row_loc, level_loc, result,
    blocks, slots, halo, coarse, fine, proj, banded, kron, acc, part,
    near, sums, far, turned, swap_out, swap_in,
    send_raw, recv_raw, send_pair, recv_pair,
    send_a, recv_a, send_x, recv_x, send_y, recv_y, send_h, recv_h,
    send_near, recv_near, send_far, recv_far, send_s, recv_s
):
    z, x, core, y = place()
    f32, bf16 = jnp.float32, jnp.bfloat16
    members, chips = blocks.shape[0], blocks.shape[1]
    columns, rows, levels = fine.shape
    coarse_rows = stencil.shape[1]
    stride = coarse_rows + 8
    kept = acc.shape[0]
    per_side = depth // 2
    count = per_side * 2
    side = lax.div(z, per_side)
    chip = z * 2 + x
    across, beside = target(z, x, core, 1 - y), target(z, 1 - x, core, y)
    partner = target(z, x, 1 - core, y)
    line = [(lax.rem(z + dz, depth), lax.rem(core + dc, 2)) for dz in range(depth) for dc in range(2)]
    greet(
        [target(zz, x, cc, y) for zz, cc in line[1:]]
        + [target(lax.rem(z + dz, depth), 1 - x, core, y) for dz in range(depth)]
        + [across, target(z, 1 - x, core, 1 - y)]
    )

    mine = lax.rem(z, per_side) * 4 + x * 2 + core
    kind = lax.rem(z, per_side) * 2 + core

    def is_self(zz):
        return jnp.logical_and(z == zz, core == side)

    for zz in range(depth):
        @pl.when(jnp.logical_not(is_self(zz)))
        def _():
            pltpu.make_async_remote_copy(
                own.at[y], slots.at[mine, y], send_a.at[zz], recv_a.at[kind],
                target(zz, x, side, y), MESH,
            ).start()

        @pl.when(is_self(zz))
        def _():
            pltpu.make_async_copy(own.at[y], slots.at[mine, y], recv_a.at[kind]).start()

    def raw_copy(m, step):
        to = lax.rem(chip + step, chips)
        return pltpu.make_async_remote_copy(
            raw.at[to * members + m], blocks.at[m, chip, core], send_raw.at[m, step],
            recv_raw.at[m, chip], target(lax.div(to, 2), lax.rem(to, 2), core, y), MESH,
        )

    def send_member(m):
        for step in range(1, chips):
            raw_copy(m, step).start()
        pltpu.make_async_copy(
            raw.at[chip * members + m], blocks.at[m, chip, core], recv_raw.at[m, chip]
        ).start()

    def pair_copy(m):
        held = blocks.at[m, :, core]
        return pltpu.make_async_remote_copy(held, held, send_pair.at[m], recv_pair.at[m], partner, MESH)

    early = min(2, members)
    for m in range(early):
        send_member(m)

    def done(ref, sem):
        pltpu.make_async_copy(ref, ref, sem).wait()

    def forward(slot, send, recv, peer):
        held = slots.at[slot, y]
        pltpu.make_async_remote_copy(held, held, send, recv, peer, MESH).start()

    for k in range(count):
        slot = (k // 2) * 4 + x * 2 + k % 2
        done(slots.at[slot, y], recv_a.at[k])
        forward(slot, send_x.at[k], recv_x.at[k], beside)
        forward(slot, send_y.at[k], recv_y.at[k], across)
    for k in range(count):
        slot = (k // 2) * 4 + (1 - x) * 2 + k % 2
        done(slots.at[slot, y], recv_x.at[k])
        forward(slot, send_y.at[count + k], recv_y.at[count + k], across)
    for m in range(early, members):
        send_member(m)
    for k in range(count):
        done(slots.at[(k // 2) * 4 + x * 2 + k % 2, 1 - y], recv_y.at[k])
    for k in range(count):
        done(slots.at[(k // 2) * 4 + (1 - x) * 2 + k % 2, 1 - y], recv_y.at[count + k])
    edges = pltpu.make_async_remote_copy(
        slots.at[(1 - core) * (2 * count - 1)], halo, send_h, recv_h, partner, MESH
    )
    edges.start()

    acc[...] = jnp.zeros_like(acc)
    tall_at = lax.broadcasted_iota(jnp.int32, (128, 8), 0)
    wide_at = lax.broadcasted_iota(jnp.int32, (128, 24 * GROUP), 1)
    deep_at = lax.broadcasted_iota(jnp.int32, (128, 24 * GROUP), 0)
    spread_rows = (tall_at // GROUP == lax.broadcasted_iota(jnp.int32, (128, 8), 1)).astype(bf16)
    spread_cols = (deep_at == wide_at // GROUP).astype(bf16)
    same = lax.rem(deep_at, GROUP) == lax.rem(wide_at, GROUP)
    for b in range(kept // 8):
        band = slots[b, 0, 4 * rows : 4 * rows + 8, :]
        tall = jnp.dot(spread_rows, band, preferred_element_type=f32).astype(bf16)
        wide = jnp.dot(tall, spread_cols, preferred_element_type=f32)
        kron[b] = jnp.where(same, wide, 0.0).astype(bf16)
    edges.wait()

    partners = [(1 - x, y), (x, 1 - y), (1 - x, 1 - y)]

    def rows_of(yy):
        return pl.ds(pl.multiple_of(yy * (rows // 2), rows // 2), rows // 2)

    def near_copy(k, n):
        xx, yy = partners[n]
        slot = lax.div(k, 2) * 4 + xx * 2 + lax.rem(k, 2)
        return pltpu.make_async_remote_copy(
            part.at[slot, :, rows_of(yy), :], near.at[n, k], send_near.at[n, k],
            recv_near.at[n, k], target(z, xx, core, yy), MESH,
        )

    def send_slot(b):
        k = lax.div(b, 4) * 2 + lax.rem(b, 2)
        inside = lax.rem(lax.div(b, 2), 2) == x

        @pl.when(inside)
        def _():
            near_copy(k, 1).start()

        @pl.when(jnp.logical_not(inside))
        def _():
            near_copy(k, 2).start()
            near_copy(k, 0).start()

    def refine(pair, table):
        base = 2 * pair * stride
        joined = jnp.concatenate(
            [coarse[pl.ds(base + k * stride, coarse_rows), :].astype(bf16) for k in range(2)], axis=1
        )
        fresh = jnp.dot(stencil[...], joined, preferred_element_type=f32).astype(bf16)
        for k in range(2):
            piece = fresh[:, k * levels : (k + 1) * levels]
            j = 2 * pair + k
            fine[j] = piece
            proj[j] = (piece.astype(f32) * table(k).astype(f32)).astype(bf16)

    @pl.loop(0, members)
    def _(m):
        for c in range(chips):
            done(blocks.at[m, c, core], recv_raw.at[m, c])
        copy = pair_copy(m)
        copy.start()
        copy.wait_recv()

        @pl.loop(0, chips)
        def _(c):
            for half in range(2):
                for two in range(2):
                    pair = jnp.concatenate(
                        [blocks[m, c, half, 2 * two], blocks[m, c, half, 2 * two + 1]], axis=1
                    )
                    mixed = jnp.dot(interp[...], pair, preferred_element_type=f32)
                    row = 8 * c + 4 * half + 2 * two
                    for k in range(2):
                        coarse[pl.ds(row + k, columns, stride=stride), :] = mixed[
                            :, k * levels : (k + 1) * levels
                        ]

        for pair in range(4):
            def table(k):
                j = 2 * pair + k
                return halo[j // 4, (j % 4) * rows : (j % 4 + 1) * rows, :]

            refine(pair, table)
            refine(columns // 2 - 4 + pair, table)

        @pl.loop(0, kept // 8)
        def _(b):
            for pair in range(4):
                def table(k):
                    j = 2 * pair + k
                    return slots[b, j // 4, (j % 4) * rows : (j % 4 + 1) * rows, :]

                refine(4 + 4 * b + pair, table)

        @pl.loop(0, kept // 8)
        def _(b):
            for pair in range(rows // (2 * GROUP)):
                parts = []
                for k in range(2):
                    at = (2 * pair + k) * GROUP
                    parts.append(proj[pl.ds(8 * b, 24), at : at + GROUP, :].reshape(24 * GROUP, levels))
                mixed = jnp.dot(
                    kron[b], jnp.concatenate(parts, axis=1), preferred_element_type=f32
                ).astype(bf16)
                for k in range(2):
                    at = (2 * pair + k) * GROUP
                    banded[:, at : at + GROUP, :] = mixed[:, k * levels : (k + 1) * levels].reshape(
                        8, GROUP, levels
                    )
            for pair in range(4):
                joined = jnp.concatenate([banded[2 * pair], banded[2 * pair + 1]], axis=1)
                mixed = jnp.dot(row_loc[...], joined, preferred_element_type=f32).astype(bf16)
                localized = jnp.dot(mixed, level_loc[...], preferred_element_type=f32)
                for k in range(2):
                    j = 8 * b + 2 * pair + k
                    acc[j] += fine[8 + j].astype(f32) * localized[:, k * levels : (k + 1) * levels]

            @pl.when(m == members - 1)
            def _():
                part[b] = acc[pl.ds(8 * b, 8)].astype(bf16)

                @pl.when(b > 0)
                def _():
                    send_slot(b - 1)

    send_slot(kept // 8 - 1)

    for k in range(count):
        for n in range(3):
            near_copy(k, n).wait_recv()
        slot = (k // 2) * 4 + x * 2 + k % 2
        total = acc[pl.ds(8 * slot, 8), rows_of(y), :]
        total = (total + near[0, k].astype(f32)) + (near[1, k].astype(f32) + near[2, k].astype(f32))
        sums[k] = total.astype(bf16)
        owner = per_side * core + k // 2
        to_self = jnp.logical_and(z == owner, core == k % 2)

        @pl.when(jnp.logical_not(to_self))
        def _():
            pltpu.make_async_remote_copy(
                sums.at[k], far.at[z], send_far.at[k], recv_far.at[z],
                target(owner, x, k % 2, y), MESH,
            ).start()

        @pl.when(to_self)
        def _():
            pltpu.make_async_copy(sums.at[k], far.at[z], recv_far.at[z]).start()

    for m in range(members):
        for step in range(1, chips):
            raw_copy(m, step).wait_send()
        pair_copy(m).wait_send()
    for k in range(count):
        done(slots.at[(k // 2) * 4 + x * 2 + k % 2, y], send_x.at[k])
    for k in range(2 * count):
        done(slots.at[k, y], send_y.at[k])
    for zz in range(depth):
        @pl.when(jnp.logical_not(is_self(zz)))
        def _():
            done(own.at[y], send_a.at[zz])

    for zz in range(depth):
        done(far.at[zz], recv_far.at[zz])

    def levels_of(yy):
        return pl.ds(pl.multiple_of(yy * (levels // 2), levels // 2), levels // 2)

    half = rows // 2
    swaps = []
    for pair in range(4):
        pieces = []
        for k in range(2):
            value = far[0, 2 * pair + k].astype(f32)
            for zz in range(1, depth):
                value = value + far[zz, 2 * pair + k].astype(f32)
            pieces.append(value)
        turned[pair] = jnp.concatenate(pieces, axis=0).T
        swap_out[pair] = turned[pair, levels_of(1 - y), :].astype(bf16)
        copy = pltpu.make_async_remote_copy(
            swap_out.at[pair], swap_in.at[pair], send_s.at[pair], recv_s.at[pair], across, MESH
        )
        copy.start()
        swaps.append(copy)
    for pair in range(4):
        swaps[pair].wait_recv()
        held = turned[pair, levels_of(y), :]
        came = swap_in[pair].astype(f32)
        low = jnp.where(y == 0, held, came)
        high = jnp.where(y == 0, came, held)
        for k in range(2):
            at = slice(k * half, (k + 1) * half)
            result[:, 2 * pair + k, :] = jnp.concatenate([low[:, at], high[:, at]], axis=1) * scale
    for copy in swaps:
        copy.wait_send()
    for k in range(count):
        for n in range(3):
            near_copy(k, n).wait_send()
        owner = per_side * core + k // 2

        @pl.when(jnp.logical_not(jnp.logical_and(z == owner, core == k % 2)))
        def _():
            done(sums.at[k], send_far.at[k])


def fused(raw, own, interp, stencil, row_loc, level_loc, depth, scale):
    bf16, f32 = jnp.bfloat16, jnp.float32
    chips = depth * 2
    members = raw.shape[0] // chips
    columns = interp.shape[0]
    rows, coarse_rows = stencil.shape
    levels = row_loc.shape[0]
    kept = columns - 16
    count = depth
    dma = pltpu.SemaphoreType.DMA
    vmem = pl.BlockSpec(memory_space=pltpu.VMEM)
    piece = (8, rows // 2, levels)
    swap = (4, levels // 2, rows)
    flops = 2 * members * levels * rows * columns * (coarse_rows + 24 * GROUP + rows + levels)
    return pl.pallas_call(
        functools.partial(fused_kernel, depth, scale),
        out_shape=jax.ShapeDtypeStruct((levels // 2, 8, rows), f32),
        in_specs=[pl.BlockSpec(memory_space=pl.ANY)] + [vmem] * 5,
        out_specs=vmem,
        scratch_shapes=[
            pltpu.VMEM((members, chips, 2) + raw.shape[1:], bf16),
            pltpu.VMEM((kept // 8,) + own.shape, bf16),
            pltpu.VMEM(own.shape, bf16),
            pltpu.VMEM((columns * (coarse_rows + 8), levels), f32),
            pltpu.VMEM((columns, rows, levels), bf16),
            pltpu.VMEM((columns, rows, levels), bf16),
            pltpu.VMEM((8, rows, levels), bf16),
            pltpu.VMEM((kept // 8, 8 * GROUP, 24 * GROUP), bf16),
            pltpu.VMEM((kept, rows, levels), f32),
            pltpu.VMEM((kept // 8, 8, rows, levels), bf16),
            pltpu.VMEM((3, count) + piece, bf16),
            pltpu.VMEM((count,) + piece, bf16),
            pltpu.VMEM((depth,) + piece, bf16),
            pltpu.VMEM((4, levels, rows), f32),
            pltpu.VMEM(swap, bf16),
            pltpu.VMEM(swap, bf16),
            dma((members, chips)), dma((members, chips)), dma((members,)), dma((members,)),
            dma((depth,)), dma((count,)), dma((count,)), dma((count,)),
            dma((2 * count,)), dma((2 * count,)), dma, dma,
            dma((3, count)), dma((3, count)), dma((count,)), dma((depth,)), dma((4,)), dma((4,)),
        ],
        compiler_params=pltpu.CompilerParams(
            collective_id=0, has_side_effects=True, vmem_limit_bytes=48 * 1024 * 1024
        ),
        cost_estimate=pl.CostEstimate(flops=flops, bytes_accessed=4 * raw.size, transcendentals=0),
    )(raw, own, interp, stencil, row_loc, level_loc)


def member_increment(
    ens_coarse, col_interp, row_weights, ctrl_vec, band_loc, row_loc, level_loc, total_members
):
    bf16 = jnp.bfloat16
    tiles = lax.axis_size("tile")
    core = lax.rem(lax.axis_index("tile"), 2)
    columns = band_loc.shape[0]
    fine_rows = row_weights.shape[1]
    levels = level_loc.shape[0]
    own = jnp.transpose(ctrl_vec[0], (1, 2, 0)).astype(bf16).reshape(2, columns // 2 * fine_rows, levels)
    band = jnp.pad(band_loc, ((0, 16 - columns), (0, levels - band_loc.shape[1])))
    own = jnp.concatenate([own, jnp.broadcast_to(band, (2,) + band.shape)], axis=1)
    stencil = row_matrix(row_weights, fine_rows, fine_rows // 2)
    kept = columns * tiles // 2
    padded = jnp.pad(col_interp, ((columns, columns), (0, 0)))
    interp = lax.dynamic_slice_in_dim(padded, core * kept, kept + 2 * columns, 0)
    mixing = jnp.kron(jnp.eye(2, dtype=bf16), level_loc.T)
    raw = jnp.transpose(ens_coarse[0], (0, 2, 3, 1))
    return fused(raw, own, interp, stencil, row_loc, mixing, tiles // 4, 1.0 / (total_members - 1))


def fits(mesh_sizes, members, columns, block_rows, fine_rows, levels):
    tiles = mesh_sizes["tile"]
    return (
        mesh_sizes["grp"] == 1
        and mesh_sizes["mem"] == 2
        and tiles % 8 == 0
        and members % (tiles // 2) == 0
        and columns == 8
        and block_rows == 4
        and fine_rows == 128
        and levels == 128
    )


def body(
    ens_coarse,
    col_interp,
    row_weights,
    ctrl_vec,
    band_loc,
    row_loc,
    level_loc,
    hx_pert,
    innov,
    obs_prec,
    obs_region,
):
    total_members = hx_pert.shape[1]
    observed = hx_pert[0]
    weighted = (observed * obs_prec[0][None, :]).astype(jnp.bfloat16)
    labels = lax.broadcasted_iota(jnp.int32, (NREG, observed.shape[1]), 0)
    member_of = obs_region[0][None, :] == labels
    masked = jnp.where(member_of[:, None, :], weighted[None], jnp.zeros((), jnp.bfloat16))
    gram_sums = jnp.einsum("rko,jo->rkj", masked, observed, preferred_element_type=jnp.float32)
    innov_rows = jnp.where(member_of, innov[0][None, :], 0.0)
    right_side = jnp.dot(
        innov_rows, weighted.astype(jnp.float32).T, precision=lax.Precision.HIGHEST
    )
    sums = jnp.concatenate([gram_sums, right_side[:, :, None]], axis=2)
    sums = swap_add(lax.psum(sums, "grp") if lax.axis_size("grp") > 1 else sums)
    sizes = {axis: lax.axis_size(axis) for axis in ("grp", "tile", "mem")}
    plan = plain_increment
    if fits(
        sizes, ens_coarse.shape[1], band_loc.shape[0], ens_coarse.shape[3], row_loc.shape[0], level_loc.shape[0]
    ):
        plan = member_increment
    increment = plan(
        ens_coarse, col_interp, row_weights, ctrl_vec, band_loc, row_loc, level_loc, total_members
    )
    own_weights = solve_weights(sums)
    weights = collect(own_weights)
    return (increment[None], weights)


def solution(mesh):
    placed = (
        P("grp", "mem", None, "tile", None),
        P(),
        P(),
        P("grp", None, "tile", None),
        P("tile", None),
        P(),
        P(),
        P("grp", None, ("tile", "mem")),
        P("grp", ("tile", "mem")),
        P("grp", ("tile", "mem")),
        P("grp", ("tile", "mem")),
    )
    return jax.shard_map(
        body,
        mesh=mesh,
        in_specs=placed,
        out_specs=(P("grp", "mem", "tile", None), P("tile", None)),
        check_vma=False,
    )
```

time: 208 us -> 159 us (0.76)
  waiting for transfers between devices: 34.4 us -> 1.22 us
  starting transfers between devices: 14.6 us -> 2.45 us
  local copies, waits for them, and re-layouts: 15.7 us -> 5.57 us
  Pallas kernels: 132 us -> 138 us
    all_to_all x2 -> x0, waiting for transfers between devices: 32.2 us -> none  [member_increment(): lax.all_to_all(piece, 'tile', split_axis=0, concat_axis=0, tiled=True)]
    all_to_all x2 -> x0, starting transfers between devices: 12 us -> none  [member_increment(): lax.all_to_all(piece, 'tile', split_axis=0, concat_axis=0, tiled=True)]
    unnamed x29 -> x19, local copies, waits for them, and re-layouts: 8.75 us -> 2.19 us
    pallas_call x4 -> x1, Pallas kernels: 121 us -> 128 us  [fused(): pl.pallas_call(functools.partial(fused_kernel, depth, scale), out_shape=j...]
    slice x2 -> x0, local copies, waits for them, and re-layouts: 2.99 us -> none  [member_increment(): piece = jnp.swapaxes(raw[:, low:high], 1, 2)]
  transfers between devices with their start and end apart: 6 -> 2, of which waited for: 2 -> 1; matrix products, arithmetic and copies ran while one was open for 9% -> 4% of each run, Pallas kernels for 36% -> 80%
where the time goes in v3:
time: 159 us
  Pallas kernels  138 us (87%)
  other arithmetic  7.68 us (5%)
  local copies, waits for them, and re-layouts  5.57 us (4%)
  matrix products  3.18 us (2%)
  starting transfers between devices  2.45 us (2%)
    pallas_call x1, Pallas kernels, fused(): pl.pallas_call(functools.partial(fused_kernel, depth, scale), out_shape=j...  128 us
    pallas_call x1, Pallas kernels, solve_weights(): pl.pallas_call(solve_kernel, out_shape=jax.ShapeDtypeStruct((regions, 8,...  10.2 us
  transfers between devices with their start and end apart: 2, of which 1 were waited for; matrix products, arithmetic and copies ran while one was open for 4% of the time, Pallas kernels for 80%

profile of v3, /device:TPU:9, one launch (start us, length us, event | category | flops | bytes accessed | tf_op | source)
XLA Modules:
  0.0 159.0 jit_solution(3856581166142948789)
XLA Ops:
  0.6 0.7 iota_compare_fusion
  1.4 1.0 fusion.5
  2.4 1.4 convolution_bitcast_fusion
  3.8 0.2 copy.19
  4.0 0.0 copy-start.4
  4.0 0.0 copy-start.7
  4.0 0.0 copy-start.3
  4.0 0.0 copy-start.6
  4.0 1.8 %fusion = f32[8,80,80]{2,1,0:T(8,128)S(1)} fusion(pred[8,2048]{1,0:T(8,128)(4,1)S(1)} %iota_compare_fusion, bf16[80,2048]{1,0:T(8,128)(2,1)S(1)} %fusion.5, bf16[1,80,2048]{2,1,0:T(8,128)(2,1)} %param.18), kind=kOutput, calls=%fused_computation | convolution fusion | flops 211025920 | bytes 876544 | tf_op jit(solution)/shard_map/rko,jo->rkj/dot_general | solution.py:556
  5.8 0.0 copy-start.2
  5.8 0.7 copy-done.2
  6.6 0.0 copy-start
  6.6 0.0 copy-start.1
  6.6 0.8 fusion.9
  7.3 1.2 collective-permute-start
  8.6 0.6 iota_shift-right-logical_fusion
  9.1 0.5 compare_and_fusion
  9.7 0.0 copy-done.4
  9.7 0.7 copy.17
  10.4 0.0 copy-done.7
  10.4 1.1 convert_bitcast_fusion
  11.5 0.9 copy.16
  12.4 0.0 copy-done.3
  12.4 0.1 copy.18
  12.5 0.2 broadcast_multiply_fusion
  12.7 0.7 pad_dynamic-slice_fusion.4.interp
  13.4 0.0 copy-done.6
  13.5 1.0 pad_maximum_fusion.own
  14.4 0.8 add_convert_fusion.stencil
  15.3 0.0 copy-done
  15.3 0.0 copy-done.1
  15.3 127.9 %shard_map.122 = f32[64,8,128]{2,1,0:T(8,128)S(1)} custom-call(bf16[40,4,64,128]{3,2,1,0:T(8,128)(2,1)S(1)} %bitcast.39, bf16[2,528,128]{2,1,0:T(8,128)(2,1)S(1)} %pad_maximum_fusion.own, bf16[80,64]{1,0:T(8,128)(2,1)S(1)} %pad_dynamic-slice_fusion.4.interp, bf16[128,64]{1,0:T(8,128)(2,1)S(1)} %add_convert_fusion.stencil, bf16[128,128]{1,0:T(8,128)(2,1)S(1)} %copy-done.1, ...), custom_call_target="tpu_custom_call" | custom-call | flops 9227468800 | bytes 5242880 | tf_op jit(solution)/shard_map/pallas_call | solution.py:468
  143.2 0.0 collective-permute-done
  143.2 1.0 fusion.11
  144.2 0.7 pad.14.sums
  144.9 10.2 %shard_map.123 = f32[4,8,128]{2,1,0:T(8,128)} custom-call(f32[4,80,128]{2,1,0:T(8,128)} %pad.14.sums), custom_call_target="tpu_custom_call" | custom-call | flops 1000000000 | bytes 163840 | tf_op jit(solution)/shard_map/pallas_call | solution.py:95
  155.1 0.7 slice.16
  155.8 1.2 collective-permute-start.1
  157.0 1.2 collective-permute-done.1
  158.2 0.0 copy-start.5
  158.2 0.7 copy.26
  159.0 0.0 copy-done.5
  (9 shorter events, 0.1 us)
Async XLA Ops:
  4.0 5.7 %copy-start.4 = (bf16[128,64]{0,1:T(8,128)(2,1)S(1)}, bf16[128,64]{0,1:T(8,128)(2,1)}, u32[]{:S(2)}) copy-start(bf16[128,64]{0,1:T(8,128)(2,1)} %param.12) | copy-start | bytes 49156
  4.0 6.4 %copy-start.7 = (bf16[3,128]{1,0:T(4,128)(2,1)S(1)}, bf16[3,128]{1,0:T(4,128)(2,1)}, u32[]{:S(2)}) copy-start(bf16[3,128]{1,0:T(4,128)(2,1)} %param.13) | copy-start | bytes 2308
  4.0 8.4 %copy-start.3 = (bf16[128,128]{1,0:T(8,128)(2,1)S(1)}, bf16[128,128]{1,0:T(8,128)(2,1)}, u32[]{:S(2)}) copy-start(bf16[128,128]{1,0:T(8,128)(2,1)} %param.17) | copy-start | bytes 98308
  4.0 9.4 %copy-start.6 = (bf16[8,24]{1,0:T(8,128)(2,1)S(1)}, bf16[8,24]{1,0:T(8,128)(2,1)}, u32[]{:S(2)}) copy-start(bf16[8,24]{1,0:T(8,128)(2,1)} %param.15) | copy-start | bytes 1156
  5.8 0.7 copy-start.2
  6.6 8.7 %copy-start = (bf16[1,40,128,4,64]{2,4,3,1,0:T(8,128)(2,1)S(1)}, bf16[1,40,128,4,64]{2,4,3,1,0:T(8,128)(2,1)}, u32[]{:S(2)}) copy-start(bf16[1,40,128,4,64]{2,4,3,1,0:T(8,128)(2,1)} %param.11) | copy-start | bytes 7864324
  6.6 8.7 %copy-start.1 = (bf16[128,128]{1,0:T(8,128)(2,1)S(1)}, bf16[128,128]{1,0:T(8,128)(2,1)}, u32[]{:S(2)}) copy-start(bf16[128,128]{1,0:T(8,128)(2,1)} %row_loc.1) | copy-start | bytes 98308
  7.3 135.8 %collective-permute-start = (f32[4,80,81]{2,1,0:T(8,128)}, f32[4,80,81]{2,1,0:T(8,128)S(1)}, u32[]{:S(2)}, u32[]{:S(2)}) collective-permute-start(f32[4,80,81]{2,1,0:T(8,128)} %fusion.9), channel_id=1, source_target_pairs={{0,1},{1,0},{2,3},{3,2},{4,5},{5,4},{6,7},{7,6},{8,9},{9,8},{10,11... | collective-permute-start | bytes 311048 | tf_op jit(solution)/shard_map/ppermute | solution.py:37
  155.8 2.4 %collective-permute-start.1 = (f32[4,80]{1,0:T(4,128)S(1)}, f32[4,80]{1,0:T(4,128)S(1)}, u32[]{:S(2)}, u32[]{:S(2)}) collective-permute-start(f32[4,80]{1,0:T(4,128)S(1)} %bitcast.45), channel_id=1, source_target_pairs={{0,1},{1,0},{2,3},{3,2},{4,5},{5,4},{6,7},{7,6},{8,9},{9,8},{10,11... | collective-permute-start | bytes 3848 | tf_op jit(solution)/shard_map/ppermute | solution.py:49
  158.2 0.7 copy-start.5

commit v4 on v3

--- a/solution.py
+++ b/solution.py
@@ -63,29 +63,28 @@
     return stencil.astype(jnp.bfloat16)
 
 
-def solve_kernel(sums, result):
-    regions, members, lanes = sums.shape
+def eliminate(tables):
+    members, lanes = tables[0].shape
     row_index = lax.broadcasted_iota(jnp.int32, (members, lanes), 0)
     col_index = lax.broadcasted_iota(jnp.int32, (members, lanes), 1)
-    tables = []
-    for region in range(regions):
-        table = sums[region]
-        square = jnp.concatenate([table, jnp.zeros((lanes - members, lanes), jnp.float32)], axis=0)
-        mirrored = square.T[:members]
+    filler = jnp.zeros((lanes - members, lanes), jnp.float32)
+    systems = []
+    for table in tables:
+        mirrored = jnp.concatenate([table, filler], axis=0).T[:members]
         table = jnp.where(col_index < members, 0.5 * (table + mirrored), table)
-        tables.append(table + jnp.where(row_index == col_index, float(members - 1), 0.0))
+        systems.append(table + jnp.where(row_index == col_index, float(members - 1), 0.0))
     for k in range(members):
-        for region in range(regions):
-            table = tables[region]
+        for region, table in enumerate(systems):
             row = table[k : k + 1]
-            pivot = row[:, k : k + 1]
-            row = row / pivot
+            row = row / row[:, k : k + 1]
             column = table[:, k : k + 1] - jnp.where(row_index[:, :1] == k, 1.0, 0.0)
-            tables[region] = table - column * row
-    for region in range(regions):
-        result[region] = jnp.concatenate(
-            [tables[region], jnp.zeros((lanes - members, lanes), jnp.float32)], axis=0
-        ).T[members : members + 8, :]
+            systems[region] = table - column * row
+    return [jnp.concatenate([table, filler], axis=0).T[members : members + 8] for table in systems]
+
+
+def solve_kernel(sums, result):
+    for region, rows in enumerate(eliminate([sums[r] for r in range(sums.shape[0])])):
+        result[region] = rows
 
 
 def solve_weights(sums):
@@ -156,12 +155,30 @@
 
 
 def fused_kernel(
-    depth, scale, raw, own, interp, stencil, row_loc, level_loc, result,
+    depth, scale, raw, *refs
+):
+    sources, refs = refs[:10], refs[10:]
+    outputs, places, refs = refs[:2], refs[2:12], refs[12:]
+    loads, refs = refs[0], refs[1:]
+    copies = [
+        pltpu.make_async_copy(source, place_in, loads.at[n])
+        for n, (source, place_in) in enumerate(zip(sources, places))
+    ]
+    for copy in copies:
+        copy.start()
+    fused_steps(depth, scale, raw, copies, *places, *outputs, *refs)
+
+
+def fused_steps(
+    depth, scale, raw, copies, ctrl, band_in, columns_in, row_weights, row_loc, levels_in,
+    observed, innov, precision, region, result, weights,
+    own, interp, stencil, level_loc, shifted, gram, gram_in, solved, solved_in,
     blocks, slots, halo, coarse, fine, proj, banded, kron, acc, part,
     near, sums, far, turned, swap_out, swap_in,
     send_raw, recv_raw, send_pair, recv_pair,
     send_a, recv_a, send_x, recv_x, send_y, recv_y, send_h, recv_h,
-    send_near, recv_near, send_far, recv_far, send_s, recv_s
+    send_near, recv_near, send_far, recv_far, send_s, recv_s,
+    send_g, recv_g, send_w, recv_w
 ):
     z, x, core, y = place()
     f32, bf16 = jnp.float32, jnp.bfloat16
@@ -176,6 +193,19 @@
     chip = z * 2 + x
     across, beside = target(z, x, core, 1 - y), target(z, 1 - x, core, y)
     partner = target(z, x, 1 - core, y)
+    copies[0].wait()
+    for j in range(8):
+        own[j // 4, (j % 4) * rows : (j % 4 + 1) * rows, :] = ctrl[:, j, :].T.astype(bf16)
+    copies[1].wait()
+    window = band_in.shape[1]
+    widen = (
+        lax.broadcasted_iota(jnp.int32, (window, levels), 0)
+        == lax.broadcasted_iota(jnp.int32, (window, levels), 1)
+    ).astype(bf16)
+    band_rows = jnp.dot(band_in[...], widen, preferred_element_type=f32)
+    band_rows = jnp.concatenate([band_rows, jnp.zeros_like(band_rows)], axis=0).astype(bf16)
+    for h in range(2):
+        own[h, 4 * rows : 4 * rows + 16, :] = band_rows
     line = [(lax.rem(z + dz, depth), lax.rem(core + dc, 2)) for dz in range(depth) for dc in range(2)]
     greet(
         [target(zz, x, cc, y) for zz, cc in line[1:]]
@@ -225,6 +255,48 @@
 
     def done(ref, sem):
         pltpu.make_async_copy(ref, ref, sem).wait()
+
+    for copy in copies[2:]:
+        copy.wait()
+    people, spots = observed.shape
+    hx = observed[...]
+    weighted = (hx.astype(f32) * precision[...]).astype(bf16).astype(f32)
+    rest = innov[...]
+    thirds = jnp.zeros((48, spots), f32)
+    third_at = lax.broadcasted_iota(jnp.int32, (48, spots), 0)
+    for n in range(3):
+        third = rest.astype(bf16).astype(f32)
+        thirds = jnp.where(third_at == n, third, thirds)
+        rest = rest - third
+    right = jnp.concatenate([hx, thirds.astype(bf16)], axis=0)
+    for g in range(NREG):
+        masked = jnp.where(region[...] == g, weighted, 0.0).astype(bf16)
+        gram[g] = lax.dot_general(
+            masked, right, (((1,), (1,)), ((), ())), preferred_element_type=f32
+        )
+    per_half = NREG // 2
+    grams = pltpu.make_async_remote_copy(
+        gram.at[pl.ds((1 - y) * per_half, per_half)], gram_in, send_g, recv_g, across, MESH
+    )
+    grams.start()
+
+    coarse_width = columns_in.shape[0]
+    fill = jnp.zeros((levels - coarse_width, levels), f32)
+    shifted[...] = jnp.zeros_like(shifted)
+    shifted[8 : 8 + levels, :] = jnp.concatenate([columns_in[...].astype(f32), fill], axis=0).T
+    interp[...] = shifted[pl.ds(pl.multiple_of(core * kept, 8), columns), :][:, :coarse_width].astype(bf16)
+    coarse_at = lax.broadcasted_iota(jnp.int32, (coarse_rows, rows), 0)
+    parent_at = lax.broadcasted_iota(jnp.int32, (coarse_rows, rows), 1) // 2
+    spreading = jnp.zeros((coarse_rows, rows), f32)
+    for n in range(3):
+        spreading = spreading + jnp.where(
+            coarse_at == parent_at + n - 1, row_weights[n : n + 1, :].astype(f32), 0.0
+        )
+    stencil[...] = jnp.concatenate([spreading, fill], axis=0).T[:, :coarse_rows].astype(bf16)
+    flipped = levels_in[...].astype(f32).T.astype(bf16)
+    level_loc[...] = jnp.zeros_like(level_loc)
+    level_loc[:levels, :levels] = flipped
+    level_loc[levels:, levels:] = flipped
 
     def forward(slot, send, recv, peer):
         held = slots.at[slot, y]
@@ -241,6 +313,11 @@
         forward(slot, send_y.at[count + k], recv_y.at[count + k], across)
     for m in range(early, members):
         send_member(m)
+    grams.wait_recv()
+    answers = eliminate([gram[y * per_half + g] + gram_in[g] for g in range(per_half)])
+    for g, rows_solved in enumerate(answers):
+        solved[g : g + 1, :] = rows_solved[0:1] + rows_solved[1:2] + rows_solved[2:3]
+    solved[per_half:, :] = jnp.zeros_like(solved[per_half:, :])
     for k in range(count):
         done(slots.at[(k // 2) * 4 + x * 2 + k % 2, 1 - y], recv_y.at[k])
     for k in range(count):
@@ -263,6 +340,8 @@
         wide = jnp.dot(tall, spread_cols, preferred_element_type=f32)
         kron[b] = jnp.where(same, wide, 0.0).astype(bf16)
     edges.wait()
+    answer = pltpu.make_async_remote_copy(solved, solved_in, send_w, recv_w, across, MESH)
+    answer.start()
 
     partners = [(1 - x, y), (x, 1 - y), (1 - x, 1 - y)]
 
@@ -395,6 +474,11 @@
         def _():
             pltpu.make_async_copy(sums.at[k], far.at[z], recv_far.at[z]).start()
 
+    answer.wait()
+    held, came = solved[:per_half, :people], solved_in[:per_half, :people]
+    weights[:per_half, :] = jnp.where(y == 0, held, came)
+    weights[per_half:, :] = jnp.where(y == 0, came, held)
+    grams.wait_send()
     for m in range(members):
         for step in range(1, chips):
             raw_copy(m, step).wait_send()
@@ -451,26 +535,48 @@
             done(sums.at[k], send_far.at[k])
 
 
-def fused(raw, own, interp, stencil, row_loc, level_loc, depth, scale):
+def fused(
+    raw, ctrl, band, columns_in, row_weights, row_loc, level_loc, observed, innov, precision, region,
+    depth, scale
+):
     bf16, f32 = jnp.bfloat16, jnp.float32
     chips = depth * 2
     members = raw.shape[0] // chips
-    columns = interp.shape[0]
-    rows, coarse_rows = stencil.shape
+    columns = 8 * chips + 16
+    coarse_rows, rows = row_weights.shape[1] // 2, row_weights.shape[1]
     levels = row_loc.shape[0]
+    people = observed.shape[0]
     kept = columns - 16
     count = depth
+    loaded = (
+        ctrl, band, columns_in, row_weights, row_loc, level_loc, observed, innov, precision, region
+    )
     dma = pltpu.SemaphoreType.DMA
     vmem = pl.BlockSpec(memory_space=pltpu.VMEM)
+    own = jax.ShapeDtypeStruct((2, 4 * rows + 16, levels), bf16)
     piece = (8, rows // 2, levels)
     swap = (4, levels // 2, rows)
     flops = 2 * members * levels * rows * columns * (coarse_rows + 24 * GROUP + rows + levels)
     return pl.pallas_call(
         functools.partial(fused_kernel, depth, scale),
-        out_shape=jax.ShapeDtypeStruct((levels // 2, 8, rows), f32),
-        in_specs=[pl.BlockSpec(memory_space=pl.ANY)] + [vmem] * 5,
-        out_specs=vmem,
+        out_shape=(
+            jax.ShapeDtypeStruct((levels // 2, 8, rows), f32),
+            jax.ShapeDtypeStruct((NREG, people), f32),
+        ),
+        in_specs=[pl.BlockSpec(memory_space=pltpu.HBM)] * 11,
+        out_specs=(vmem, vmem),
         scratch_shapes=[
+            *[pltpu.VMEM(value.shape, value.dtype) for value in loaded],
+            dma((len(loaded),)),
+            pltpu.VMEM(own.shape, bf16),
+            pltpu.VMEM((columns, raw.shape[2]), bf16),
+            pltpu.VMEM((rows, coarse_rows), bf16),
+            pltpu.VMEM((2 * levels, 2 * levels), bf16),
+            pltpu.VMEM((2 * kept + 16, levels), f32),
+            pltpu.VMEM((NREG, people, 128), f32),
+            pltpu.VMEM((NREG // 2, people, 128), f32),
+            pltpu.VMEM((8, 128), f32),
+            pltpu.VMEM((8, 128), f32),
             pltpu.VMEM((members, chips, 2) + raw.shape[1:], bf16),
             pltpu.VMEM((kept // 8,) + own.shape, bf16),
             pltpu.VMEM(own.shape, bf16),
@@ -491,42 +597,49 @@
             dma((depth,)), dma((count,)), dma((count,)), dma((count,)),
             dma((2 * count,)), dma((2 * count,)), dma, dma,
             dma((3, count)), dma((3, count)), dma((count,)), dma((depth,)), dma((4,)), dma((4,)),
+            dma, dma, dma, dma,
         ],
         compiler_params=pltpu.CompilerParams(
             collective_id=0, has_side_effects=True, vmem_limit_bytes=48 * 1024 * 1024
         ),
         cost_estimate=pl.CostEstimate(flops=flops, bytes_accessed=4 * raw.size, transcendentals=0),
-    )(raw, own, interp, stencil, row_loc, level_loc)
-
-
-def member_increment(
-    ens_coarse, col_interp, row_weights, ctrl_vec, band_loc, row_loc, level_loc, total_members
+    )(raw, *loaded)
+
+
+def member_plan(
+    ens_coarse,
+    col_interp,
+    row_weights,
+    ctrl_vec,
+    band_loc,
+    row_loc,
+    level_loc,
+    hx_pert,
+    innov,
+    obs_prec,
+    obs_region,
 ):
-    bf16 = jnp.bfloat16
-    tiles = lax.axis_size("tile")
-    core = lax.rem(lax.axis_index("tile"), 2)
-    columns = band_loc.shape[0]
-    fine_rows = row_weights.shape[1]
-    levels = level_loc.shape[0]
-    own = jnp.transpose(ctrl_vec[0], (1, 2, 0)).astype(bf16).reshape(2, columns // 2 * fine_rows, levels)
-    band = jnp.pad(band_loc, ((0, 16 - columns), (0, levels - band_loc.shape[1])))
-    own = jnp.concatenate([own, jnp.broadcast_to(band, (2,) + band.shape)], axis=1)
-    stencil = row_matrix(row_weights, fine_rows, fine_rows // 2)
-    kept = columns * tiles // 2
-    padded = jnp.pad(col_interp, ((columns, columns), (0, 0)))
-    interp = lax.dynamic_slice_in_dim(padded, core * kept, kept + 2 * columns, 0)
-    mixing = jnp.kron(jnp.eye(2, dtype=bf16), level_loc.T)
     raw = jnp.transpose(ens_coarse[0], (0, 2, 3, 1))
-    return fused(raw, own, interp, stencil, row_loc, mixing, tiles // 4, 1.0 / (total_members - 1))
-
-
-def fits(mesh_sizes, members, columns, block_rows, fine_rows, levels):
+    increment, weights = fused(
+        raw, ctrl_vec[0], band_loc, col_interp.T, row_weights, row_loc, level_loc,
+        hx_pert[0], innov, obs_prec, obs_region,
+        lax.axis_size("tile") // 4, 1.0 / (hx_pert.shape[1] - 1),
+    )
+    return (increment[None], weights)
+
+
+def fits(mesh_sizes, total_members, block, columns, fine_rows, levels):
     tiles = mesh_sizes["tile"]
+    members, block_rows, width = block[1], block[3], block[4]
     return (
         mesh_sizes["grp"] == 1
         and mesh_sizes["mem"] == 2
         and tiles % 8 == 0
         and members % (tiles // 2) == 0
+        and tiles * columns == levels
+        and width <= levels
+        and total_members % 8 == 0
+        and total_members + 48 == levels
         and columns == 8
         and block_rows == 4
         and fine_rows == 128
@@ -547,7 +660,13 @@
     obs_prec,
     obs_region,
 ):
+    sizes = {axis: lax.axis_size(axis) for axis in ("grp", "tile", "mem")}
     total_members = hx_pert.shape[1]
+    if fits(sizes, total_members, ens_coarse.shape, band_loc.shape[0], row_loc.shape[0], level_loc.shape[0]):
+        return member_plan(
+            ens_coarse, col_interp, row_weights, ctrl_vec, band_loc, row_loc, level_loc,
+            hx_pert, innov, obs_prec, obs_region,
+        )
     observed = hx_pert[0]
     weighted = (observed * obs_prec[0][None, :]).astype(jnp.bfloat16)
     labels = lax.broadcasted_iota(jnp.int32, (NREG, observed.shape[1]), 0)
@@ -560,13 +679,7 @@
     )
     sums = jnp.concatenate([gram_sums, right_side[:, :, None]], axis=2)
     sums = swap_add(lax.psum(sums, "grp") if lax.axis_size("grp") > 1 else sums)
-    sizes = {axis: lax.axis_size(axis) for axis in ("grp", "tile", "mem")}
-    plan = plain_increment
-    if fits(
-        sizes, ens_coarse.shape[1], band_loc.shape[0], ens_coarse.shape[3], row_loc.shape[0], level_loc.shape[0]
-    ):
-        plan = member_increment
-    increment = plan(
+    increment = plain_increment(
         ens_coarse, col_interp, row_weights, ctrl_vec, band_loc, row_loc, level_loc, total_members
     )
     own_weights = solve_weights(sums)

time: 159 us -> 142 us (0.89)
  Pallas kernels: 138 us -> 129 us
  other arithmetic: 7.68 us -> 0 us
  local copies, waits for them, and re-layouts: 5.57 us -> 10.7 us
  matrix products: 3.18 us -> 0 us
  starting transfers between devices: 2.45 us -> 0 us
    pallas_call x2 -> x1, Pallas kernels: 138 us -> 129 us  [fused(): pl.pallas_call(functools.partial(fused_kernel, depth, scale), out_shape=(...]
    unnamed x19 -> x24, local copies, waits for them, and re-layouts: 2.19 us -> 10.7 us
    dot_general x2 -> x0, matrix products: 3.18 us -> none  [the longest x1 1.81 us: body(): jnp.einsum('rko,jo->rkj', masked, observed, preferred_element_type=jnp.fl...]
    ppermute x2 -> x0, starting transfers between devices: 2.45 us -> none  [the longest x1 1.24 us: swap_add(): total = total + lax.ppermute(part, 'mem', pairs)]
    convert_element_type x4 -> x0, other arithmetic: 1.91 us -> none  [the longest x1 1.07 us: member_increment(): jnp.transpose(ctrl_vec[0], (1, 2, 0)).astype(bf16)]
    concatenate x2 -> x0, other arithmetic: 1.76 us -> none  [the longest x1 0.97 us: member_increment(): jnp.concatenate([own, jnp.broadcast_to(band, (2,) + band.shape)], axis=1)]
  transfers between devices with their start and end apart: 2 -> 0, of which waited for: 1 -> 0; matrix products, arithmetic and copies ran while one was open for 4% -> 0% of each run, Pallas kernels for 80% -> 0%
where the time goes in v4:
time: 142 us; the launch traced here: 141 us
  Pallas kernels  129 us (91%)
  local copies, waits for them, and re-layouts  10.7 us (8%)
    pallas_call x1, Pallas kernels, fused(): pl.pallas_call(functools.partial(fused_kernel, depth, scale), out_shape=(...  129 us
    unnamed x24, local copies, waits for them, and re-layouts  10.7 us

profile of v4, /device:TPU:9, one launch (start us, length us, event | category | flops | bytes accessed | tf_op | source)
XLA Modules:
  0.0 140.6 jit_solution(18097835397497827439)
XLA Ops:
  0.6 0.0 copy-start
  0.6 1.7 %copy-done = bf16[1,40,128,4,64]{2,4,3,1,0:T(8,128)(2,1)S(1)} copy-done((bf16[1,40,128,4,64]{2,4,3,1,0:T(8,128)(2,1)S(1)}, bf16[1,40,128,4,64]{2,4,3,1,0:T(8,128)(2,1)}, u32[]{:S(2)}) %copy-start) | copy-done | bytes 2621464
  2.4 0.0 copy-start.1
  2.4 1.0 copy-done.1
  3.4 0.0 copy-start.2
  3.4 1.0 copy-done.2
  4.4 0.0 copy-start.3
  4.4 0.8 copy-done.3
  5.1 0.0 copy-start.4
  5.2 0.8 copy-done.4
  5.9 0.0 copy-start.5
  5.9 0.7 copy-done.5
  6.6 0.0 copy-start.6
  6.6 0.7 copy-done.6
  7.3 0.0 copy-start.7
  7.3 0.7 copy-done.7
  8.0 0.0 copy-start.8
  8.0 0.7 copy-done.8
  8.7 0.0 copy-start.9
  8.7 0.7 copy-done.9
  9.4 0.0 copy-start.10
  9.4 0.7 copy-done.10
  10.1 129.3 %shard_map.122 = (f32[64,8,128]{2,1,0:T(8,128)S(1)}, f32[8,80]{1,0:T(8,128)S(1)}) custom-call(bf16[40,4,64,128]{3,2,1,0:T(8,128)(2,1)S(1)} %bitcast.8, f32[128,8,128]{2,1,0:T(8,128)S(1)} %bitcast.9, bf16[8,24]{1,0:T(8,128)(2,1)S(1)} %copy-done.9, bf16[64,128]{1,0:T(8,128)(2,1)S(1)} %bitcast.11, bf16[3,128]{1,0:T(4,128)(2,1)S(1)} %copy-done.10, ...), custom_call_target="tpu_custom_call" | custom-call | flops 9227468800 | bytes 5242880 | tf_op jit(solution)/shard_map/pallas_call | solution.py:560
  139.3 0.7 copy.15
  140.0 0.6 copy.16
Async XLA Ops:
  0.6 1.7 %copy-start = (bf16[1,40,128,4,64]{2,4,3,1,0:T(8,128)(2,1)S(1)}, bf16[1,40,128,4,64]{2,4,3,1,0:T(8,128)(2,1)}, u32[]{:S(2)}) copy-start(bf16[1,40,128,4,64]{2,4,3,1,0:T(8,128)(2,1)} %param.11) | copy-start | bytes 7864324
  2.4 1.0 copy-start.1
  3.4 1.0 copy-start.2
  4.4 0.8 copy-start.3
  5.1 0.8 copy-start.4
  5.9 0.7 copy-start.5
  6.6 0.7 copy-start.6
  7.3 0.7 copy-start.7
  8.0 0.7 copy-start.8
  8.7 0.7 copy-start.9
  9.4 0.7 copy-start.10

commit v5 on v4

--- a/solution.py
+++ b/solution.py
@@ -389,8 +389,7 @@
         copy.start()
         copy.wait_recv()
 
-        @pl.loop(0, chips)
-        def _(c):
+        for c in range(chips):
             for half in range(2):
                 for two in range(2):
                     pair = jnp.concatenate(
@@ -411,8 +410,7 @@
             refine(pair, table)
             refine(columns // 2 - 4 + pair, table)
 
-        @pl.loop(0, kept // 8)
-        def _(b):
+        for b in range(kept // 8):
             for pair in range(4):
                 def table(k):
                     j = 2 * pair + k
@@ -420,37 +418,47 @@
 
                 refine(4 + 4 * b + pair, table)
 
-        @pl.loop(0, kept // 8)
-        def _(b):
+        def band_mix(b):
             for pair in range(rows // (2 * GROUP)):
                 parts = []
                 for k in range(2):
                     at = (2 * pair + k) * GROUP
-                    parts.append(proj[pl.ds(8 * b, 24), at : at + GROUP, :].reshape(24 * GROUP, levels))
+                    parts.append(proj[8 * b : 8 * b + 24, at : at + GROUP, :].reshape(24 * GROUP, levels))
                 mixed = jnp.dot(
                     kron[b], jnp.concatenate(parts, axis=1), preferred_element_type=f32
                 ).astype(bf16)
                 for k in range(2):
                     at = (2 * pair + k) * GROUP
-                    banded[:, at : at + GROUP, :] = mixed[:, k * levels : (k + 1) * levels].reshape(
-                        8, GROUP, levels
-                    )
+                    banded[b % 2, :, at : at + GROUP, :] = mixed[
+                        :, k * levels : (k + 1) * levels
+                    ].reshape(8, GROUP, levels)
+
+        def level_mix(b):
             for pair in range(4):
-                joined = jnp.concatenate([banded[2 * pair], banded[2 * pair + 1]], axis=1)
+                joined = jnp.concatenate(
+                    [banded[b % 2, 2 * pair], banded[b % 2, 2 * pair + 1]], axis=1
+                )
                 mixed = jnp.dot(row_loc[...], joined, preferred_element_type=f32).astype(bf16)
                 localized = jnp.dot(mixed, level_loc[...], preferred_element_type=f32)
                 for k in range(2):
                     j = 8 * b + 2 * pair + k
                     acc[j] += fine[8 + j].astype(f32) * localized[:, k * levels : (k + 1) * levels]
 
+        for b in range(0, kept // 8, 2):
+            band_mix(b)
+            band_mix(b + 1)
+            level_mix(b)
+            level_mix(b + 1)
+
             @pl.when(m == members - 1)
             def _():
-                part[b] = acc[pl.ds(8 * b, 8)].astype(bf16)
-
-                @pl.when(b > 0)
-                def _():
+                for slot in (b, b + 1):
+                    part[slot] = acc[8 * slot : 8 * slot + 8].astype(bf16)
+                if b > 0:
+                    send_slot(b - 2)
                     send_slot(b - 1)
 
+    send_slot(kept // 8 - 2)
     send_slot(kept // 8 - 1)
 
     for k in range(count):
@@ -583,7 +591,7 @@
             pltpu.VMEM((columns * (coarse_rows + 8), levels), f32),
             pltpu.VMEM((columns, rows, levels), bf16),
             pltpu.VMEM((columns, rows, levels), bf16),
-            pltpu.VMEM((8, rows, levels), bf16),
+            pltpu.VMEM((2, 8, rows, levels), bf16),
             pltpu.VMEM((kept // 8, 8 * GROUP, 24 * GROUP), bf16),
             pltpu.VMEM((kept, rows, levels), f32),
             pltpu.VMEM((kept // 8, 8, rows, levels), bf16),
@@ -600,7 +608,7 @@
             dma, dma, dma, dma,
         ],
         compiler_params=pltpu.CompilerParams(
-            collective_id=0, has_side_effects=True, vmem_limit_bytes=48 * 1024 * 1024
+            collective_id=0, has_side_effects=True, vmem_limit_bytes=67043328
         ),
         cost_estimate=pl.CostEstimate(flops=flops, bytes_accessed=4 * raw.size, transcendentals=0),
     )(raw, *loaded)

time: 142 us -> 121 us (0.85)
  Pallas kernels: 129 us -> 117 us
  local copies, waits for them, and re-layouts: 10.7 us -> 2.95 us
    pallas_call x1, Pallas kernels: 129 us -> 117 us  [fused(): pl.pallas_call(functools.partial(fused_kernel, depth, scale), out_shape=(...]
    unnamed x24 -> x2, local copies, waits for them, and re-layouts: 10.7 us -> 2.95 us
where the time goes in v5:
time: 121 us
  Pallas kernels  117 us (97%)
  local copies, waits for them, and re-layouts  2.95 us (2%)
    pallas_call x1, Pallas kernels, fused(): pl.pallas_call(functools.partial(fused_kernel, depth, scale), out_shape=(...  117 us
    unnamed x2, local copies, waits for them, and re-layouts  2.95 us

profile of v5, /device:TPU:9, one launch (start us, length us, event | category | flops | bytes accessed | tf_op | source)
XLA Modules:
  0.0 121.0 jit_solution(6848706712438218084)
XLA Ops:
  0.6 117.4 %shard_map.122 = (f32[64,8,128]{2,1,0:T(8,128)}, f32[8,80]{1,0:T(8,128)}) custom-call(bf16[40,4,64,128]{3,2,1,0:T(8,128)(2,1)} %bitcast.8, f32[128,8,128]{2,1,0:T(8,128)} %bitcast.9, bf16[8,24]{1,0:T(8,128)(2,1)} %refs_1_.1, bf16[64,128]{1,0:T(8,128)(2,1)} %bitcast.11, bf16[3,128]{1,0:T(4,128)(2,1)} %refs_3_.1, bf16[128,128]{1,0:T(8,128)(2,1)} %refs_4_.1, ...), custom_call_target="tpu_custom_call" | custom-call | flops 9227468800 | bytes 5242880 | tf_op jit(solution)/shard_map/pallas_call | solution.py:568
  118.0 1.7 %copy.15 = f32[1,64,8,128]{3,2,1,0:T(8,128)} copy(f32[1,64,8,128]{3,2,1,0:T(8,128)} %bitcast.7) | data formatting | bytes 524288
  119.7 1.3 %copy.16 = f32[8,80]{1,0:T(8,128)} copy(f32[8,80]{1,0:T(8,128)} %get-tuple-element.9) | data formatting | bytes 5120

commit v6 on v5

--- a/solution.py
+++ b/solution.py
@@ -174,11 +174,11 @@
     observed, innov, precision, region, result, weights,
     own, interp, stencil, level_loc, shifted, gram, gram_in, solved, solved_in,
     blocks, slots, halo, coarse, fine, proj, banded, kron, acc, part,
-    near, sums, far, turned, swap_out, swap_in,
+    first, mid, second, sums, far,
     send_raw, recv_raw, send_pair, recv_pair,
     send_a, recv_a, send_x, recv_x, send_y, recv_y, send_h, recv_h,
-    send_near, recv_near, send_far, recv_far, send_s, recv_s,
-    send_g, recv_g, send_w, recv_w
+    send_first, recv_first, send_second, recv_second, send_far, recv_far,
+    send_g, recv_g, send_w, recv_w, send_z
 ):
     z, x, core, y = place()
     f32, bf16 = jnp.float32, jnp.bfloat16
@@ -219,8 +219,19 @@
     def is_self(zz):
         return jnp.logical_and(z == zz, core == side)
 
+    def is_gate(zz):
+        return zz == per_side - 1 + zz // per_side
+
+    def direct(zz):
+        near_side = True if is_gate(zz) else side == zz // per_side
+        return jnp.logical_and(jnp.logical_not(is_self(zz)), near_side)
+
+    def relays(zz):
+        here = jnp.logical_and(side == zz // per_side, side != core)
+        return jnp.logical_and(here, z == per_side - 1 + side)
+
     for zz in range(depth):
-        @pl.when(jnp.logical_not(is_self(zz)))
+        @pl.when(direct(zz))
         def _():
             pltpu.make_async_remote_copy(
                 own.at[y], slots.at[mine, y], send_a.at[zz], recv_a.at[kind],
@@ -305,6 +316,12 @@
     for k in range(count):
         slot = (k // 2) * 4 + x * 2 + k % 2
         done(slots.at[slot, y], recv_a.at[k])
+        for zz in range(depth):
+            if not is_gate(zz):
+                @pl.when(relays(zz))
+                def _():
+                    forward(slot, send_z.at[k, zz], recv_a.at[k], target(zz, x, core, y))
+
         forward(slot, send_x.at[k], recv_x.at[k], beside)
         forward(slot, send_y.at[k], recv_y.at[k], across)
     for k in range(count):
@@ -343,31 +360,37 @@
     answer = pltpu.make_async_remote_copy(solved, solved_in, send_w, recv_w, across, MESH)
     answer.start()
 
-    partners = [(1 - x, y), (x, 1 - y), (1 - x, 1 - y)]
-
-    def rows_of(yy):
-        return pl.ds(pl.multiple_of(yy * (rows // 2), rows // 2), rows // 2)
-
-    def near_copy(k, n):
-        xx, yy = partners[n]
-        slot = lax.div(k, 2) * 4 + xx * 2 + lax.rem(k, 2)
+    def slot_of(k, xx):
+        return (k // 2) * 4 + xx * 2 + k % 2
+
+    def first_copies(k, only=None):
+        if k % 2 == 0:
+            pieces = [(part.at[slot_of(k, 1 - x)], first.at[k], beside)]
+        else:
+            pieces = [(part.at[slot_of(k, xx), 1 - y], first.at[k, xx], across) for xx in range(2)]
+        if only is not None:
+            pieces = pieces[only : only + 1]
+        return [
+            pltpu.make_async_remote_copy(
+                source, landing, send_first.at[k, n], recv_first.at[k, n], peer, MESH
+            )
+            for n, (source, landing, peer) in enumerate(pieces, only or 0)
+        ]
+
+    def second_copy(k):
+        peer = across if k % 2 == 0 else beside
         return pltpu.make_async_remote_copy(
-            part.at[slot, :, rows_of(yy), :], near.at[n, k], send_near.at[n, k],
-            recv_near.at[n, k], target(z, xx, core, yy), MESH,
+            mid.at[k], second.at[k], send_second.at[k], recv_second.at[k], peer, MESH
         )
 
     def send_slot(b):
-        k = lax.div(b, 4) * 2 + lax.rem(b, 2)
-        inside = lax.rem(lax.div(b, 2), 2) == x
-
-        @pl.when(inside)
-        def _():
-            near_copy(k, 1).start()
-
-        @pl.when(jnp.logical_not(inside))
-        def _():
-            near_copy(k, 2).start()
-            near_copy(k, 0).start()
+        k, xx = (b // 4) * 2 + b % 2, (b // 2) % 2
+        if k % 2 == 1:
+            first_copies(k, xx)[0].start()
+        else:
+            @pl.when(x != xx)
+            def _():
+                first_copies(k)[0].start()
 
     def refine(pair, table):
         base = 2 * pair * stride
@@ -387,10 +410,8 @@
             done(blocks.at[m, c, core], recv_raw.at[m, c])
         copy = pair_copy(m)
         copy.start()
-        copy.wait_recv()
-
-        for c in range(chips):
-            for half in range(2):
+        def interpolate(half):
+            for c in range(chips):
                 for two in range(2):
                     pair = jnp.concatenate(
                         [blocks[m, c, half, 2 * two], blocks[m, c, half, 2 * two + 1]], axis=1
@@ -401,6 +422,10 @@
                         coarse[pl.ds(row + k, columns, stride=stride), :] = mixed[
                             :, k * levels : (k + 1) * levels
                         ]
+
+        interpolate(core)
+        copy.wait_recv()
+        interpolate(1 - core)
 
         for pair in range(4):
             def table(k):
@@ -453,7 +478,13 @@
             @pl.when(m == members - 1)
             def _():
                 for slot in (b, b + 1):
-                    part[slot] = acc[8 * slot : 8 * slot + 8].astype(bf16)
+                    for pair in range(4):
+                        two = [acc[8 * slot + 2 * pair + k] for k in range(2)]
+                        for h in range(2):
+                            at = slice(h * levels // 2, (h + 1) * levels // 2)
+                            part[slot, h, pair] = jnp.concatenate(
+                                [value[:, at] for value in two], axis=1
+                            ).astype(bf16)
                 if b > 0:
                     send_slot(b - 2)
                     send_slot(b - 1)
@@ -461,13 +492,21 @@
     send_slot(kept // 8 - 2)
     send_slot(kept // 8 - 1)
 
-    for k in range(count):
-        for n in range(3):
-            near_copy(k, n).wait_recv()
-        slot = (k // 2) * 4 + x * 2 + k % 2
-        total = acc[pl.ds(8 * slot, 8), rows_of(y), :]
-        total = (total + near[0, k].astype(f32)) + (near[1, k].astype(f32) + near[2, k].astype(f32))
-        sums[k] = total.astype(bf16)
+    def step_first(k):
+        for copy in first_copies(k):
+            copy.wait_recv()
+        if k % 2 == 0:
+            total = part[slot_of(k, x), 1 - y].astype(f32) + first[k, 1 - y].astype(f32)
+        else:
+            total = part[slot_of(k, 1 - x), y].astype(f32) + first[k, 1 - x].astype(f32)
+        mid[k] = total.astype(bf16)
+        second_copy(k).start()
+
+    def step_second(k):
+        second_copy(k).wait_recv()
+        kept_at = y if k % 2 == 0 else x
+        total = part[slot_of(k, x), y].astype(f32) + first[k, kept_at].astype(f32)
+        sums[k] = (total + second[k].astype(f32)).astype(bf16)
         owner = per_side * core + k // 2
         to_self = jnp.logical_and(z == owner, core == k % 2)
 
@@ -481,6 +520,12 @@
         @pl.when(to_self)
         def _():
             pltpu.make_async_copy(sums.at[k], far.at[z], recv_far.at[z]).start()
+
+    for k in range(0, count, 2):
+        step_first(k)
+        step_first(k + 1)
+        step_second(k)
+        step_second(k + 1)
 
     answer.wait()
     held, came = solved[:per_half, :people], solved_in[:per_half, :people]
@@ -496,46 +541,31 @@
     for k in range(2 * count):
         done(slots.at[k, y], send_y.at[k])
     for zz in range(depth):
-        @pl.when(jnp.logical_not(is_self(zz)))
+        @pl.when(direct(zz))
         def _():
             done(own.at[y], send_a.at[zz])
 
+        if not is_gate(zz):
+            @pl.when(relays(zz))
+            def _():
+                for k in range(count):
+                    done(own.at[y], send_z.at[k, zz])
+
     for zz in range(depth):
         done(far.at[zz], recv_far.at[zz])
 
-    def levels_of(yy):
-        return pl.ds(pl.multiple_of(yy * (levels // 2), levels // 2), levels // 2)
-
-    half = rows // 2
-    swaps = []
+    half = levels // 2
     for pair in range(4):
-        pieces = []
+        value = far[0, pair].astype(f32)
+        for zz in range(1, depth):
+            value = value + far[zz, pair].astype(f32)
+        value = value.T * scale
         for k in range(2):
-            value = far[0, 2 * pair + k].astype(f32)
-            for zz in range(1, depth):
-                value = value + far[zz, 2 * pair + k].astype(f32)
-            pieces.append(value)
-        turned[pair] = jnp.concatenate(pieces, axis=0).T
-        swap_out[pair] = turned[pair, levels_of(1 - y), :].astype(bf16)
-        copy = pltpu.make_async_remote_copy(
-            swap_out.at[pair], swap_in.at[pair], send_s.at[pair], recv_s.at[pair], across, MESH
-        )
-        copy.start()
-        swaps.append(copy)
-    for pair in range(4):
-        swaps[pair].wait_recv()
-        held = turned[pair, levels_of(y), :]
-        came = swap_in[pair].astype(f32)
-        low = jnp.where(y == 0, held, came)
-        high = jnp.where(y == 0, came, held)
-        for k in range(2):
-            at = slice(k * half, (k + 1) * half)
-            result[:, 2 * pair + k, :] = jnp.concatenate([low[:, at], high[:, at]], axis=1) * scale
-    for copy in swaps:
-        copy.wait_send()
+            result[:, 2 * pair + k, :] = value[k * half : (k + 1) * half]
     for k in range(count):
-        for n in range(3):
-            near_copy(k, n).wait_send()
+        for copy in first_copies(k):
+            copy.wait_send()
+        second_copy(k).wait_send()
         owner = per_side * core + k // 2
 
         @pl.when(jnp.logical_not(jnp.logical_and(z == owner, core == k % 2)))
@@ -562,8 +592,7 @@
     dma = pltpu.SemaphoreType.DMA
     vmem = pl.BlockSpec(memory_space=pltpu.VMEM)
     own = jax.ShapeDtypeStruct((2, 4 * rows + 16, levels), bf16)
-    piece = (8, rows // 2, levels)
-    swap = (4, levels // 2, rows)
+    piece = (4, rows, levels)
     flops = 2 * members * levels * rows * columns * (coarse_rows + 24 * GROUP + rows + levels)
     return pl.pallas_call(
         functools.partial(fused_kernel, depth, scale),
@@ -594,18 +623,17 @@
             pltpu.VMEM((2, 8, rows, levels), bf16),
             pltpu.VMEM((kept // 8, 8 * GROUP, 24 * GROUP), bf16),
             pltpu.VMEM((kept, rows, levels), f32),
-            pltpu.VMEM((kept // 8, 8, rows, levels), bf16),
-            pltpu.VMEM((3, count) + piece, bf16),
+            pltpu.VMEM((kept // 8, 2) + piece, bf16),
+            pltpu.VMEM((count, 2) + piece, bf16),
+            pltpu.VMEM((count,) + piece, bf16),
+            pltpu.VMEM((count,) + piece, bf16),
             pltpu.VMEM((count,) + piece, bf16),
             pltpu.VMEM((depth,) + piece, bf16),
-            pltpu.VMEM((4, levels, rows), f32),
-            pltpu.VMEM(swap, bf16),
-            pltpu.VMEM(swap, bf16),
             dma((members, chips)), dma((members, chips)), dma((members,)), dma((members,)),
             dma((depth,)), dma((count,)), dma((count,)), dma((count,)),
             dma((2 * count,)), dma((2 * count,)), dma, dma,
-            dma((3, count)), dma((3, count)), dma((count,)), dma((depth,)), dma((4,)), dma((4,)),
-            dma, dma, dma, dma,
+            dma((count, 2)), dma((count, 2)), dma((count,)), dma((count,)), dma((count,)), dma((depth,)),
+            dma, dma, dma, dma, dma((count, depth)),
         ],
         compiler_params=pltpu.CompilerParams(
             collective_id=0, has_side_effects=True, vmem_limit_bytes=67043328

time: 121 us -> 115 us (0.950)
  Pallas kernels: 117 us -> 111 us
    pallas_call x1, Pallas kernels: 117 us -> 111 us  [fused(): pl.pallas_call(functools.partial(fused_kernel, depth, scale), out_shape=(...]
where the time goes in v6:
time: 115 us
  Pallas kernels  111 us (97%)
  local copies, waits for them, and re-layouts  2.95 us (3%)
    pallas_call x1, Pallas kernels, fused(): pl.pallas_call(functools.partial(fused_kernel, depth, scale), out_shape=(...  111 us
    unnamed x2, local copies, waits for them, and re-layouts  2.95 us

profile of v6, /device:TPU:9, one launch (start us, length us, event | category | flops | bytes accessed | tf_op | source)
XLA Modules:
  0.0 114.7 jit_solution(13064773050761704553)
XLA Ops:
  0.6 111.1 %shard_map.122 = (f32[64,8,128]{2,1,0:T(8,128)}, f32[8,80]{1,0:T(8,128)}) custom-call(bf16[40,4,64,128]{3,2,1,0:T(8,128)(2,1)} %bitcast.8, f32[128,8,128]{2,1,0:T(8,128)} %bitcast.9, bf16[8,24]{1,0:T(8,128)(2,1)} %refs_1_.1, bf16[64,128]{1,0:T(8,128)(2,1)} %bitcast.11, bf16[3,128]{1,0:T(4,128)(2,1)} %refs_3_.1, bf16[128,128]{1,0:T(8,128)(2,1)} %refs_4_.1, ...), custom_call_target="tpu_custom_call" | custom-call | flops 9227468800 | bytes 5242880 | tf_op jit(solution)/shard_map/pallas_call | solution.py:597
  111.8 1.7 %copy.15 = f32[1,64,8,128]{3,2,1,0:T(8,128)} copy(f32[1,64,8,128]{3,2,1,0:T(8,128)} %bitcast.7) | data formatting | bytes 524288
  113.4 1.3 %copy.16 = f32[8,80]{1,0:T(8,128)} copy(f32[8,80]{1,0:T(8,128)} %get-tuple-element.9) | data formatting | bytes 5120

commit v7 on v6

--- a/solution.py
+++ b/solution.py
@@ -75,9 +75,9 @@
         systems.append(table + jnp.where(row_index == col_index, float(members - 1), 0.0))
     for k in range(members):
         for region, table in enumerate(systems):
-            row = table[k : k + 1]
-            row = row / row[:, k : k + 1]
-            column = table[:, k : k + 1] - jnp.where(row_index[:, :1] == k, 1.0, 0.0)
+            column = jnp.broadcast_to(table[:, k : k + 1], table.shape)
+            row = table[k : k + 1] * (1.0 / column[k : k + 1])
+            column = jnp.where(row_index == k, column - 1.0, column)
             systems[region] = table - column * row
     return [jnp.concatenate([table, filler], axis=0).T[members : members + 8] for table in systems]
 

time: 115 us -> 113 us (0.983)
  Pallas kernels: 111 us -> 109 us
    pallas_call x1, Pallas kernels: 111 us -> 109 us  [fused(): pl.pallas_call(functools.partial(fused_kernel, depth, scale), out_shape=(...]
where the time goes in v7:
time: 113 us
  Pallas kernels  109 us (96%)
  local copies, waits for them, and re-layouts  2.95 us (3%)
    pallas_call x1, Pallas kernels, fused(): pl.pallas_call(functools.partial(fused_kernel, depth, scale), out_shape=(...  109 us
    unnamed x2, local copies, waits for them, and re-layouts  2.95 us

profile of v7, /device:TPU:9, one launch (start us, length us, event | category | flops | bytes accessed | tf_op | source)
XLA Modules:
  0.0 113.0 jit_solution(14363791986374119543)
XLA Ops:
  0.6 109.4 %shard_map.122 = (f32[64,8,128]{2,1,0:T(8,128)}, f32[8,80]{1,0:T(8,128)}) custom-call(bf16[40,4,64,128]{3,2,1,0:T(8,128)(2,1)} %bitcast.8, f32[128,8,128]{2,1,0:T(8,128)} %bitcast.9, bf16[8,24]{1,0:T(8,128)(2,1)} %refs_1_.1, bf16[64,128]{1,0:T(8,128)(2,1)} %bitcast.11, bf16[3,128]{1,0:T(4,128)(2,1)} %refs_3_.1, bf16[128,128]{1,0:T(8,128)(2,1)} %refs_4_.1, ...), custom_call_target="tpu_custom_call" | custom-call | flops 9227468800 | bytes 5242880 | tf_op jit(solution)/shard_map/pallas_call | solution.py:597
  110.0 1.7 %copy.15 = f32[1,64,8,128]{3,2,1,0:T(8,128)} copy(f32[1,64,8,128]{3,2,1,0:T(8,128)} %bitcast.7) | data formatting | bytes 524288
  111.7 1.3 %copy.16 = f32[8,80]{1,0:T(8,128)} copy(f32[8,80]{1,0:T(8,128)} %get-tuple-element.9) | data formatting | bytes 5120
